TPU v7x, 32 devices: a 4x4x1 block of a 4x4x8 slice. The times are simulated.
32 devices in a mesh: dp: 1 (over z), u: 4 (over y), r: 8 (over x, core).
Axes of the slice: x: 4, y: 4, z: 1, core: 2. Of those that a mesh axis runs over, the one named last changes fastest.
The devices are a block of a 4x4x8 slice.
Arguments:
- image: bfloat16 [8, 2048, 1536], P('dp', ('r', 'u'))
- text: bfloat16 [8, 160, 1536], P('dp', ('r', 'u'))
- cond_vec: bfloat16 [8, 1536], P('dp')
- key_valid: int32 [8, 160], P('dp')
- w_mod: bfloat16 [2, 2, 1536, 9216], replicated
- b_mod: bfloat16 [2, 2, 9216], replicated
- w_qkv: bfloat16 [2, 2, 1536, 4608], replicated
- b_qkv: bfloat16 [2, 2, 4608], replicated
- q_gain: bfloat16 [2, 2, 24, 64], replicated
- k_gain: bfloat16 [2, 2, 24, 64], replicated
- w_proj: bfloat16 [2, 2, 1536, 1536], replicated
- b_proj: bfloat16 [2, 2, 1536], replicated
- w_up: bfloat16 [2, 2, 1536, 6144], replicated
- b_up: bfloat16 [2, 2, 6144], replicated
- w_down: bfloat16 [2, 2, 6144, 1536], replicated
- b_down: bfloat16 [2, 2, 1536], replicated
Outputs:
- output 1: bfloat16 [8, 2048, 1536], P('dp', ('r', 'u'))
- output 2: bfloat16 [8, 160, 1536], P('dp', ('r', 'u'))
All inputs are finite; a program needn't handle non-finite values.
Results may differ from a plain program's by a relative error of at most 0.0131662.
Values are sent between devices in bfloat16 or wider.
A program may use at most 768 MiB of HBM per device.

v0:
```python
import jax
import jax.numpy as jnp
from jax import lax
from jax.sharding import PartitionSpec as P

EPSILON = 1e-6
MASK_FILL = -1e30


def modulated_norm(hidden, shift, scale):
    wide = hidden.astype(jnp.float32)
    centered = wide - jnp.mean(wide, axis=-1, keepdims=True)
    variance = jnp.mean(centered * centered, axis=-1, keepdims=True)
    return ((1.0 + scale) * (centered * lax.rsqrt(variance + EPSILON)) + shift).astype(jnp.bfloat16)


def head_norm(heads_f32, gain):
    mean_sq = jnp.mean(heads_f32 * heads_f32, axis=-1, keepdims=True)
    return (heads_f32 * lax.rsqrt(mean_sq + EPSILON) * gain.astype(jnp.float32)).astype(jnp.bfloat16)


def linear(rows, weight, bias):
    return jnp.einsum('bld,de->ble', rows, weight, preferred_element_type=jnp.float32) + bias.astype(jnp.float32)


def modulation(silu_vec, w_mod, b_mod):
    mod_vecs = jnp.dot(silu_vec, w_mod, preferred_element_type=jnp.float32) + b_mod.astype(jnp.float32)
    return mod_vecs.reshape(silu_vec.shape[0], 6, 1, w_mod.shape[0])


def modality_qkv(hidden, mod_vecs, w_qkv, b_qkv, q_gain, k_gain):
    normed = modulated_norm(hidden, mod_vecs[:, 0], mod_vecs[:, 1])
    packed = linear(normed, w_qkv, b_qkv)
    packed = packed.reshape(hidden.shape[0], hidden.shape[1], 3, q_gain.shape[0], q_gain.shape[1])
    return head_norm(packed[:, :, 0], q_gain), head_norm(packed[:, :, 1], k_gain), packed[:, :, 2].astype(jnp.bfloat16)


def modality_out(hidden, attended, mod_vecs, w_proj, b_proj, w_up, b_up, w_down, b_down):
    residual = hidden.astype(jnp.float32) + mod_vecs[:, 2] * linear(attended, w_proj, b_proj)
    hidden = residual.astype(jnp.bfloat16)
    normed = modulated_norm(hidden, mod_vecs[:, 3], mod_vecs[:, 4])
    inner = jax.nn.gelu(linear(normed, w_up, b_up), approximate=True).astype(jnp.bfloat16)
    return (hidden.astype(jnp.float32) + mod_vecs[:, 5] * linear(inner, w_down, b_down)).astype(jnp.bfloat16)


def sample_attention(operands):
    query, keys, values, key_bias = operands
    scores = jnp.einsum('qhd,khd->hqk', query, keys, preferred_element_type=jnp.float32) * query.shape[-1] ** -0.5 + key_bias
    attn_prob = jax.nn.softmax(scores, axis=-1).astype(jnp.bfloat16)
    return jnp.einsum('hqk,khd->qhd', attn_prob, values, preferred_element_type=jnp.float32).astype(jnp.bfloat16)


def solution(mesh):
    seq_spec = P('dp', ('r', 'u'), None)
    row_spec = P('dp', None)
    head_ways = mesh.shape['u']
    group_size = mesh.shape['u'] * mesh.shape['r']

    def local_blocks(image, text, cond_vec, key_valid, w_mod, b_mod, w_qkv, b_qkv, q_gain, k_gain, w_proj, b_proj, w_up, b_up, w_down, b_down):
        batch = image.shape[0]
        silu_vec = jax.nn.silu(cond_vec.astype(jnp.float32)).astype(jnp.bfloat16)
        text_bias = jnp.where(key_valid > 0, 0.0, MASK_FILL).astype(jnp.float32)
        key_bias = jnp.concatenate([text_bias, jnp.zeros((batch, image.shape[1] * group_size), jnp.float32)], axis=1)
        text_rows = text.shape[1] * head_ways
        for block in range(w_mod.shape[0]):
            sides = [image, text]
            mod_list = [modulation(silu_vec, w_mod[block, side], b_mod[block, side]) for side in range(2)]
            by_heads = []
            for side in range(2):
                projected = modality_qkv(sides[side], mod_list[side], w_qkv[block, side], b_qkv[block, side], q_gain[block, side], k_gain[block, side])
                by_heads.append([lax.all_to_all(tensor, 'u', 2, 1, tiled=True) for tensor in projected])
            keys_all = jnp.concatenate([lax.all_gather(by_heads[1][1], 'r', axis=1, tiled=True), lax.all_gather(by_heads[0][1], 'r', axis=1, tiled=True)], axis=1)
            values_all = jnp.concatenate([lax.all_gather(by_heads[1][2], 'r', axis=1, tiled=True), lax.all_gather(by_heads[0][2], 'r', axis=1, tiled=True)], axis=1)
            queries = jnp.concatenate([by_heads[1][0], by_heads[0][0]], axis=1)
            attended = lax.map(sample_attention, (queries, keys_all, values_all, key_bias))
            head_parts = [attended[:, text_rows:], attended[:, :text_rows]]
            new_sides = []
            for side in range(2):
                tokens_out = lax.all_to_all(head_parts[side], 'u', 1, 2, tiled=True)
                tokens_out = tokens_out.reshape(batch, tokens_out.shape[1], -1)
                new_sides.append(modality_out(sides[side], tokens_out, mod_list[side], w_proj[block, side], b_proj[block, side], w_up[block, side], b_up[block, side], w_down[block, side], b_down[block, side]))
            image, text = new_sides
        return image, text

    return jax.shard_map(local_blocks, mesh=mesh, in_specs=(seq_spec, seq_spec, row_spec, row_spec) + (P(),) * 12, out_specs=(seq_spec, seq_spec), check_vma=False)
```

profile of v0, /device:TPU:97, one launch (start us, length us, event | category | flops | bytes accessed | tf_op | source)
XLA Modules:
  0.0 1406.9 jit_solution(16656817100730103917)
XLA Ops:
  8.8 11.1 fusion.112
  22.3 13.4 fusion.132
  35.7 14.6 %reshape.335 = f32[8,64,3,24,64]{4,3,2,1,0:T(8,128)} reshape(f32[8,64,4608]{2,1,0:T(8,128)} %fusion.132) | data formatting | bytes 18874368 | tf_op jit(solution)/shard_map/reshape | solution.py:34
  74.5 26.4 %all_to_all.276 = bf16[4,2,98304]{2,1,0:T(2,128)(2,1)} all-to-all(bf16[4,2,98304]{2,1,0:T(2,128)(2,1)S(1)} %reshape.410), channel_id=1, replica_groups=mesh['dp'=1,'u'=4,'r'=8] {'u'}, dimensions={0} | all-to-all | bytes 3145728 | tf_op jit(solution)/shard_map/all_to_all | solution.py:71
  121.6 23.3 %all_to_all.277 = bf16[4,2,98304]{2,1,0:T(2,128)(2,1)} all-to-all(bf16[4,2,98304]{2,1,0:T(2,128)(2,1)} %reshape.402), channel_id=1, replica_groups=mesh['dp'=1,'u'=4,'r'=8] {'u'}, dimensions={0} | all-to-all | bytes 3145728 | tf_op jit(solution)/shard_map/all_to_all | solution.py:71
  158.5 11.0 fusion.115
  198.5 11.1 fusion.118
  220.9 36.4 %all_gather.26 = bf16[8,160,6,64]{3,0,2,1:T(8,128)(2,1)S(1)} all-gather(bf16[8,20,6,64]{3,0,2,1:T(8,128)(2,1)S(1)} %bitcast.606), channel_id=1, replica_groups=mesh['dp'=1,'u'=4,'r'=8] {'r'}, dimensions={1}, use_global_device_ids=true | all-gather | bytes 1105920 | tf_op jit(solution)/shard_map/all_gather | solution.py:72
  262.8 24.0 %all_gather.24 = bf16[8,160,6,64]{3,0,2,1:T(8,128)(2,1)S(1)} all-gather(bf16[8,20,6,64]{3,0,2,1:T(8,128)(2,1)S(1)} %bitcast.609), channel_id=1, replica_groups=mesh['dp'=1,'u'=4,'r'=8] {'r'}, dimensions={1}, use_global_device_ids=true | all-gather | bytes 1105920 | tf_op jit(solution)/shard_map/all_gather | solution.py:73
  306.1 14.1 %pad_maximum_fusion.1 = bf16[8,2208,6,64]{1,3,2,0:T(8,128)(2,1)} fusion(bf16[8,2048,6,64]{1,3,2,0:T(8,128)(2,1)} %all-gather.7.cloned.1.call-done, bf16[8,160,6,64]{1,3,2,0:T(8,128)(2,1)S(1)} %copy-done.5), kind=kLoop, calls=%fused_computation.83 | loop fusion | flops 27131904 | bytes 27131904 | tf_op jit(solution)/shard_map/concatenate | solution.py:72
  320.2 14.0 pad_maximum_fusion
  334.6 283.8 %while.20 = (s32[]{:T(128)}, bf16[8,276,6,64]{1,3,2,0:T(8,128)(2,1)S(1)}, bf16[8,2208,6,64]{1,3,2,0:T(8,128)(2,1)}, bf16[8,276,6,64]{1,3,2,0:T(8,128)(2,1)}, bf1...) while((s32[]{:T(128)}, bf16[8,276,6,64]{1,3,2,0:T(8,128)(2,1)S(1)}, ...), condition=%wide.region_11.12_spmd, body=%wide.region_8.11_spmd.sunk | while | flops 965410432 | bytes 63536560 | solution.py:75
  343.9 17.6 %fusion.500 = (f32[6,276]{1,0:T(8,128)S(1)}, f32[6,276,2208]{2,1,0:T(8,128)}) fusion(f32[6,276,2208]{2,1,0:T(8,128)} %fusion.499, f32[2208]{0:T(1024)S(1)} %dynamic-slice_reduce_fusion.4), kind=kOutput, calls=%fused_computation.430.clone.1 | output fusion | flops 21940896 | bytes 29267040 | tf_op jit(solution)/shard_map/while/body/eval_jaxpr/sub | solution.py:49
  370.1 9.3 fusion.499
  379.4 17.6 %fusion.500 = (f32[6,276]{1,0:T(8,128)S(1)}, f32[6,276,2208]{2,1,0:T(8,128)}) fusion(f32[6,276,2208]{2,1,0:T(8,128)} %fusion.499, f32[2208]{0:T(1024)S(1)} %dynamic-slice_reduce_fusion.4), kind=kOutput, calls=%fused_computation.430.clone.1 | output fusion | flops 21940896 | bytes 29267040 | tf_op jit(solution)/shard_map/while/body/eval_jaxpr/sub | solution.py:49
  414.8 17.6 %fusion.500 = (f32[6,276]{1,0:T(8,128)S(1)}, f32[6,276,2208]{2,1,0:T(8,128)}) fusion(f32[6,276,2208]{2,1,0:T(8,128)} %fusion.499, f32[2208]{0:T(1024)S(1)} %dynamic-slice_reduce_fusion.4), kind=kOutput, calls=%fused_computation.430.clone.1 | output fusion | flops 21940896 | bytes 29267040 | tf_op jit(solution)/shard_map/while/body/eval_jaxpr/sub | solution.py:49
  450.3 17.6 %fusion.500 = (f32[6,276]{1,0:T(8,128)S(1)}, f32[6,276,2208]{2,1,0:T(8,128)}) fusion(f32[6,276,2208]{2,1,0:T(8,128)} %fusion.499, f32[2208]{0:T(1024)S(1)} %dynamic-slice_reduce_fusion.4), kind=kOutput, calls=%fused_computation.430.clone.1 | output fusion | flops 21940896 | bytes 29267040 | tf_op jit(solution)/shard_map/while/body/eval_jaxpr/sub | solution.py:49
  485.8 17.6 %fusion.500 = (f32[6,276]{1,0:T(8,128)S(1)}, f32[6,276,2208]{2,1,0:T(8,128)}) fusion(f32[6,276,2208]{2,1,0:T(8,128)} %fusion.499, f32[2208]{0:T(1024)S(1)} %dynamic-slice_reduce_fusion.4), kind=kOutput, calls=%fused_computation.430.clone.1 | output fusion | flops 21940896 | bytes 29267040 | tf_op jit(solution)/shard_map/while/body/eval_jaxpr/sub | solution.py:49
  512.0 9.3 fusion.499
  521.3 17.6 %fusion.500 = (f32[6,276]{1,0:T(8,128)S(1)}, f32[6,276,2208]{2,1,0:T(8,128)}) fusion(f32[6,276,2208]{2,1,0:T(8,128)} %fusion.499, f32[2208]{0:T(1024)S(1)} %dynamic-slice_reduce_fusion.4), kind=kOutput, calls=%fused_computation.430.clone.1 | output fusion | flops 21940896 | bytes 29267040 | tf_op jit(solution)/shard_map/while/body/eval_jaxpr/sub | solution.py:49
  556.8 17.6 %fusion.500 = (f32[6,276]{1,0:T(8,128)S(1)}, f32[6,276,2208]{2,1,0:T(8,128)}) fusion(f32[6,276,2208]{2,1,0:T(8,128)} %fusion.499, f32[2208]{0:T(1024)S(1)} %dynamic-slice_reduce_fusion.4), kind=kOutput, calls=%fused_computation.430.clone.1 | output fusion | flops 21940896 | bytes 29267040 | tf_op jit(solution)/shard_map/while/body/eval_jaxpr/sub | solution.py:49
  592.2 17.6 %fusion.500 = (f32[6,276]{1,0:T(8,128)S(1)}, f32[6,276,2208]{2,1,0:T(8,128)}) fusion(f32[6,276,2208]{2,1,0:T(8,128)} %fusion.499, f32[2208]{0:T(1024)S(1)} %dynamic-slice_reduce_fusion.4), kind=kOutput, calls=%fused_computation.430.clone.1 | output fusion | flops 21940896 | bytes 29267040 | tf_op jit(solution)/shard_map/while/body/eval_jaxpr/sub | solution.py:49
  638.2 13.7 all-to-all-done.6
  670.3 17.0 %fusion.103.clone.7.clone.5 = bf16[8,64,6144]{2,1,0:T(8,128)(2,1)S(1)} fusion(bf16[2,2,1536,6144]{3,2,1,0:T(8,128)(2,1)} %param.32, f32[6144]{0:T(1024)S(1)} %bitcast.627, bf16[8,64,1536]{2,1,0:T(8,128)(2,1)S(1)} %get-tuple-element.157, f32[8,1536]{1,0:T(8,128)S(1)} %copy-done.35, ...), kind=kOutput, calls=%fused_computation.105.clone.clone.clone.clone.clone.clone.clone.clone.clone.clon... | convolution fusion | flops 9699852288 | bytes 26865664 | tf_op jit(solution)/shard_map/bld,de->ble/dot_general | solution.py:23
  687.3 14.5 %convert_reduce_fusion.1 = (f32[8,64]{1,0:T(8,128)S(1)}, bf16[8,64,1536]{2,1,0:T(8,128)(2,1)S(1)}) fusion(f32[1536]{0:T(1024)S(1)} %copy-done.60, bf16[2,2,6144,1536]{3,2,1,0:T(8,128)(2,1)} %param.34, bf16[8,64,1536]{2,1,0:T(8,128)(2,1)S(1)} %get-tuple-element.157, f32[8,1536]{1,0:T(8,128)S(1)} %copy-done.34, ...), kind=kOutput, calls=%fused_computation.153 | convolution fusion | flops 9669181440 | bytes 28368896 | tf_op jit(solution)/shard_map/bld,de->ble/dot_general | solution.py:23
  703.0 13.4 fusion.135
  716.4 14.6 %reshape.341 = f32[8,64,3,24,64]{4,3,2,1,0:T(8,128)} reshape(f32[8,64,4608]{2,1,0:T(8,128)} %fusion.135) | data formatting | bytes 18874368 | tf_op jit(solution)/shard_map/reshape | solution.py:34
  748.3 16.9 %all_to_all.278 = bf16[4,2,98304]{2,1,0:T(2,128)(2,1)} all-to-all(bf16[4,2,98304]{2,1,0:T(2,128)(2,1)S(1)} %reshape.426), channel_id=1, replica_groups=mesh['dp'=1,'u'=4,'r'=8] {'u'}, dimensions={0} | all-to-all | bytes 3145728 | tf_op jit(solution)/shard_map/all_to_all | solution.py:71
  786.0 16.7 %all_to_all.279 = bf16[4,2,98304]{2,1,0:T(2,128)(2,1)} all-to-all(bf16[4,2,98304]{2,1,0:T(2,128)(2,1)} %reshape.416), channel_id=1, replica_groups=mesh['dp'=1,'u'=4,'r'=8] {'u'}, dimensions={0} | all-to-all | bytes 3145728 | tf_op jit(solution)/shard_map/all_to_all | solution.py:71
  816.1 11.0 fusion.121
  841.0 15.6 %fusion.447 = (f32[8,5]{0,1:T(8,128)S(1)}, f32[8,5,1536]{2,0,1:T(8,128)S(1)}) fusion(f32[8,5,1536]{2,0,1:T(8,128)S(1)} %get-tuple-element.161, f32[1536]{0:T(1024)S(1)} %copy-done.58, bf16[2,2,6144,1536]{3,2,1,0:T(8,128)(2,1)} %param.34, bf16[2,2,1536,6144]{3,2,1,0:T(8,128)(2,1)} %param.32, f32[6144]{0:T(1024)S(1)} %bitcast.626, ...), kind=kOutput, calls=%fused_computation.437 | convolution fusion | flops 1513082880 | bytes 38674592 | tf_op jit(solution)/shard_map/bld,de->ble/dot_general | solution.py:23
  901.6 33.9 %all_gather.30 = bf16[8,160,6,64]{3,0,2,1:T(8,128)(2,1)S(1)} all-gather(bf16[8,20,6,64]{3,0,2,1:T(8,128)(2,1)S(1)} %bitcast.613), channel_id=1, replica_groups=mesh['dp'=1,'u'=4,'r'=8] {'r'}, dimensions={1}, use_global_device_ids=true | all-gather | bytes 1105920 | tf_op jit(solution)/shard_map/all_gather | solution.py:72
  940.2 25.5 %all_gather.28 = bf16[8,160,6,64]{3,0,2,1:T(8,128)(2,1)S(1)} all-gather(bf16[8,20,6,64]{3,0,2,1:T(8,128)(2,1)S(1)} %bitcast.616), channel_id=1, replica_groups=mesh['dp'=1,'u'=4,'r'=8] {'r'}, dimensions={1}, use_global_device_ids=true | all-gather | bytes 1105920 | tf_op jit(solution)/shard_map/all_gather | solution.py:73
  985.0 14.1 %pad_maximum_fusion.3 = bf16[8,2208,6,64]{1,3,2,0:T(8,128)(2,1)} fusion(bf16[8,2048,6,64]{1,3,2,0:T(8,128)(2,1)} %all-gather.11.cloned.1.call-done, bf16[8,160,6,64]{1,3,2,0:T(8,128)(2,1)S(1)} %copy-done.6), kind=kLoop, calls=%fused_computation.85 | loop fusion | flops 27131904 | bytes 27131904 | tf_op jit(solution)/shard_map/concatenate | solution.py:72
  999.1 14.0 pad_maximum_fusion.2
  1013.5 290.9 %while.21 = (s32[]{:T(128)}, bf16[8,276,6,64]{1,3,2,0:T(8,128)(2,1)S(1)}, bf16[8,2208,6,64]{1,3,2,0:T(8,128)(2,1)}, bf16[8,276,6,64]{1,3,2,0:T(8,128)(2,1)}, bf1...) while((s32[]{:T(128)}, bf16[8,276,6,64]{1,3,2,0:T(8,128)(2,1)S(1)}, ...), condition=%wide.region_27.28_spmd, body=%wide.region_24.27_spmd.sunk | while | flops 965410432 | bytes 63536560 | solution.py:75
  1023.7 17.6 %fusion.506 = (f32[6,276]{1,0:T(8,128)S(1)}, f32[6,276,2208]{2,1,0:T(8,128)}) fusion(f32[6,276,2208]{2,1,0:T(8,128)} %fusion.505, f32[2208]{0:T(1024)S(1)} %dynamic-slice_reduce_fusion.5), kind=kOutput, calls=%fused_computation.431.clone.1 | output fusion | flops 21940896 | bytes 29267040 | tf_op jit(solution)/shard_map/while/body/eval_jaxpr/sub | solution.py:49
  1060.1 17.6 %fusion.506 = (f32[6,276]{1,0:T(8,128)S(1)}, f32[6,276,2208]{2,1,0:T(8,128)}) fusion(f32[6,276,2208]{2,1,0:T(8,128)} %fusion.505, f32[2208]{0:T(1024)S(1)} %dynamic-slice_reduce_fusion.5), kind=kOutput, calls=%fused_computation.431.clone.1 | output fusion | flops 21940896 | bytes 29267040 | tf_op jit(solution)/shard_map/while/body/eval_jaxpr/sub | solution.py:49
  1096.4 17.6 %fusion.506 = (f32[6,276]{1,0:T(8,128)S(1)}, f32[6,276,2208]{2,1,0:T(8,128)}) fusion(f32[6,276,2208]{2,1,0:T(8,128)} %fusion.505, f32[2208]{0:T(1024)S(1)} %dynamic-slice_reduce_fusion.5), kind=kOutput, calls=%fused_computation.431.clone.1 | output fusion | flops 21940896 | bytes 29267040 | tf_op jit(solution)/shard_map/while/body/eval_jaxpr/sub | solution.py:49
  1132.8 17.6 %fusion.506 = (f32[6,276]{1,0:T(8,128)S(1)}, f32[6,276,2208]{2,1,0:T(8,128)}) fusion(f32[6,276,2208]{2,1,0:T(8,128)} %fusion.505, f32[2208]{0:T(1024)S(1)} %dynamic-slice_reduce_fusion.5), kind=kOutput, calls=%fused_computation.431.clone.1 | output fusion | flops 21940896 | bytes 29267040 | tf_op jit(solution)/shard_map/while/body/eval_jaxpr/sub | solution.py:49
  1159.0 9.3 fusion.505
  1169.2 17.6 %fusion.506 = (f32[6,276]{1,0:T(8,128)S(1)}, f32[6,276,2208]{2,1,0:T(8,128)}) fusion(f32[6,276,2208]{2,1,0:T(8,128)} %fusion.505, f32[2208]{0:T(1024)S(1)} %dynamic-slice_reduce_fusion.5), kind=kOutput, calls=%fused_computation.431.clone.1 | output fusion | flops 21940896 | bytes 29267040 | tf_op jit(solution)/shard_map/while/body/eval_jaxpr/sub | solution.py:49
  1205.5 17.6 %fusion.506 = (f32[6,276]{1,0:T(8,128)S(1)}, f32[6,276,2208]{2,1,0:T(8,128)}) fusion(f32[6,276,2208]{2,1,0:T(8,128)} %fusion.505, f32[2208]{0:T(1024)S(1)} %dynamic-slice_reduce_fusion.5), kind=kOutput, calls=%fused_computation.431.clone.1 | output fusion | flops 21940896 | bytes 29267040 | tf_op jit(solution)/shard_map/while/body/eval_jaxpr/sub | solution.py:49
  1241.9 17.6 %fusion.506 = (f32[6,276]{1,0:T(8,128)S(1)}, f32[6,276,2208]{2,1,0:T(8,128)}) fusion(f32[6,276,2208]{2,1,0:T(8,128)} %fusion.505, f32[2208]{0:T(1024)S(1)} %dynamic-slice_reduce_fusion.5), kind=kOutput, calls=%fused_computation.431.clone.1 | output fusion | flops 21940896 | bytes 29267040 | tf_op jit(solution)/shard_map/while/body/eval_jaxpr/sub | solution.py:49
  1278.3 17.6 %fusion.506 = (f32[6,276]{1,0:T(8,128)S(1)}, f32[6,276,2208]{2,1,0:T(8,128)}) fusion(f32[6,276,2208]{2,1,0:T(8,128)} %fusion.505, f32[2208]{0:T(1024)S(1)} %dynamic-slice_reduce_fusion.5), kind=kOutput, calls=%fused_computation.431.clone.1 | output fusion | flops 21940896 | bytes 29267040 | tf_op jit(solution)/shard_map/while/body/eval_jaxpr/sub | solution.py:49
  1334.0 15.7 %fusion.294 = bf16[8,5,1536]{2,0,1:T(8,128)(2,1)} fusion(f32[8,5,1536]{2,0,1:T(8,128)S(1)} %get-tuple-element.167, bf16[2,2,6144,1536]{3,2,1,0:T(8,128)(2,1)} %param.34, bf16[2,2,1536,6144]{3,2,1,0:T(8,128)(2,1)} %param.32, f32[6144]{0:T(1024)S(1)} %bitcast.625, f32[1536]{0:T(1024)S(1)} %copy-done.56, f32[8,1536]{1,0:T(8,128)S(1)} %copy-done.39, ...), kind=kOutput, calls=%fused_computation.230 | convolution fusion | flops 1512960000 | bytes 38551552 | tf_op jit(solution)/shard_map/bld,de->ble/dot_general | solution.py:23
  1368.1 17.2 %fusion.111.clone.11 = bf16[8,64,6144]{2,1,0:T(8,128)(2,1)S(1)} fusion(bf16[2,2,1536,6144]{3,2,1,0:T(8,128)(2,1)} %param.32, f32[6144]{0:T(1024)S(1)} %bitcast.624, bf16[8,64,1536]{2,1,0:T(8,128)(2,1)S(1)} %get-tuple-element.165, f32[8,1536]{1,0:T(8,128)S(1)} %copy-done.27, ...), kind=kOutput, calls=%fused_computation.113.clone.clone.clone.clone.clone.clone.clone.clone.clone.2 | convolution fusion | flops 9699852288 | bytes 26865664 | tf_op jit(solution)/shard_map/bld,de->ble/dot_general | solution.py:23
  1385.3 14.8 %fusion.231 = bf16[8,64,1536]{2,1,0:T(8,128)(2,1)} fusion(bf16[8,64,1536]{2,1,0:T(8,128)(2,1)S(1)} %get-tuple-element.165, bf16[2,2,6144,1536]{3,2,1,0:T(8,128)(2,1)} %param.34, f32[1536]{0:T(1024)S(1)} %copy-done.54, f32[8,1536]{1,0:T(8,128)S(1)} %copy-done.26, bf16[8,64,6144]{2,1,0:T(8,128)(2,1)S(1)} %fusion.111.clone.11), kind=kOutput, calls=%fused_computation.209 | convolution fusion | flops 9667608576 | bytes 28366848 | tf_op jit(solution)/shard_map/bld,de->ble/dot_general | solution.py:23
  (361 shorter events, 613.9 us)
Async XLA Ops:
  7.2 298.9 %all-gather.7.cloned.1.call-start = ((), (), s32[]{:S(2)}) async-start(), calls=%async_computation.17 | async-start | bytes 14155776 | tf_op jit(solution)/shard_map/all_gather | solution.py:72
  8.8 11.8 copy-start.23
  8.8 12.6 copy-start.9
  114.1 206.1 %all-gather.5.cloned.1.call-start = ((), (), s32[]{:S(2)}) async-start(), calls=%async_computation.16 | async-start | bytes 14155776 | tf_op jit(solution)/shard_map/all_gather | solution.py:73
  148.7 9.5 copy-start.13
  148.7 9.8 copy-start.11
  178.6 7.9 all-to-all-start.4
  186.5 11.9 copy-start.15
  186.5 7.9 all-to-all-start.2
  194.4 18.6 %all-to-all-start = ((bf16[4,2,7680]{2,1,0:T(2,128)(2,1)}), bf16[4,2,7680]{2,1,0:T(2,128)(2,1)}, u32[]{:S(2)}, u32[]{:S(2)}) async-start(bf16[4,2,7680]{2,1,0:T(2,128)(2,1)} %reshape.404), calls=%async_computation | async-start | bytes 245760 | tf_op jit(solution)/shard_map/all_to_all | solution.py:71
  198.5 11.2 copy-start.2
  213.0 47.0 %copy-start.17 = (bf16[4,2,7680]{2,1,0:T(2,128)(2,1)S(1)}, bf16[4,2,7680]{2,1,0:T(2,128)(2,1)}, u32[]{:S(2)}) copy-start(bf16[4,2,7680]{2,1,0:T(2,128)(2,1)} %copy-done.16) | copy-start | bytes 368644
  213.0 76.9 %all-to-all-start.3 = ((bf16[4,2,98304]{2,1,0:T(2,128)(2,1)}), bf16[4,2,98304]{2,1,0:T(2,128)(2,1)}, u32[]{:S(2)}, u32[]{:S(2)}) async-start(bf16[4,2,98304]{2,1,0:T(2,128)(2,1)} %reshape.406), calls=%async_computation.3 | async-start | bytes 3145728 | tf_op jit(solution)/shard_map/all_to_all | solution.py:71
  306.1 14.1 %copy-start.7 = (bf16[8,160,6,64]{1,3,2,0:T(8,128)(2,1)S(1)}, bf16[8,160,6,64]{1,3,2,0:T(8,128)(2,1)}, u32[]{:S(2)}) copy-start(bf16[8,160,6,64]{1,3,2,0:T(8,128)(2,1)} %copy.156) | copy-start | bytes 2949124
  619.8 12.9 copy-start.18
  625.0 12.5 copy-start.21
  632.8 19.1 %all-to-all-start.6 = ((bf16[4,2,98304]{2,1,0:T(2,128)(2,1)}), bf16[4,2,98304]{2,1,0:T(2,128)(2,1)}, u32[]{:S(2)}, u32[]{:S(2)}) async-start(bf16[4,2,98304]{2,1,0:T(2,128)(2,1)} %reshape.414), calls=%async_computation.6 | async-start | bytes 3145728 | tf_op jit(solution)/shard_map/all_to_all | solution.py:79
  637.5 347.6 %all-gather.11.cloned.1.call-start = ((), (), s32[]{:S(2)}) async-start(), calls=%async_computation.19 | async-start | bytes 14155776 | tf_op jit(solution)/shard_map/all_gather | solution.py:72
  670.3 17.0 %copy-start.34 = (f32[8,1536]{1,0:T(8,128)S(1)}, f32[8,1536]{1,0:T(8,128)}, u32[]{:S(2)}) copy-start(f32[8,1536]{1,0:T(8,128)} %get-tuple-element.134) | copy-start | bytes 147460
  670.3 17.0 %copy-start.60 = (f32[1536]{0:T(1024)S(1)}, f32[1536]{0:T(1024)}, u32[]{:S(2)}) copy-start(f32[1536]{0:T(1024)} %get-tuple-element.74) | copy-start | bytes 18436
  687.3 15.7 %copy-start.42 = (f32[8,1536]{1,0:T(8,128)S(1)}, f32[8,1536]{1,0:T(8,128)}, u32[]{:S(2)}) copy-start(f32[8,1536]{1,0:T(8,128)} %get-tuple-element.125) | copy-start | bytes 147460
  687.3 15.7 %copy-start.43 = (f32[8,1536]{1,0:T(8,128)S(1)}, f32[8,1536]{1,0:T(8,128)}, u32[]{:S(2)}) copy-start(f32[8,1536]{1,0:T(8,128)} %get-tuple-element.126) | copy-start | bytes 147460
  687.3 15.7 %copy-start.53 = (f32[4608]{0:T(1024)S(1)}, f32[4608]{0:T(1024)}, u32[]{:S(2)}) copy-start(f32[4608]{0:T(1024)} %get-tuple-element.71) | copy-start | bytes 55300
  778.5 220.6 %all-gather.9.cloned.1.call-start = ((), (), s32[]{:S(2)}) async-start(), calls=%async_computation.18 | async-start | bytes 14155776 | tf_op jit(solution)/shard_map/all_gather | solution.py:73
  806.5 9.5 copy-start.12
  806.5 9.5 copy-start.22
  816.0 21.4 %copy-start.14 = (bf16[8,5,1536]{2,0,1:T(8,128)(2,1)S(1)}, bf16[8,5,1536]{2,0,1:T(8,128)(2,1)}, u32[]{:S(2)}) copy-start(bf16[8,5,1536]{2,0,1:T(8,128)(2,1)} %param.21) | copy-start | bytes 368644
  816.1 21.4 %copy-start.33 = (f32[8,1536]{1,0:T(8,128)S(1)}, f32[8,1536]{1,0:T(8,128)}, u32[]{:S(2)}) copy-start(f32[8,1536]{1,0:T(8,128)} %get-tuple-element.131) | copy-start | bytes 147460
  816.1 21.4 %copy-start.59 = (f32[1536]{0:T(1024)S(1)}, f32[1536]{0:T(1024)}, u32[]{:S(2)}) copy-start(f32[1536]{0:T(1024)} %get-tuple-element.77) | copy-start | bytes 18436
  827.1 13.9 copy-start.30
  827.1 13.9 copy-start.31
  827.1 13.9 copy-start.32
  827.1 13.9 copy-start.58
  829.0 7.9 all-to-all-start.7
  841.0 16.3 %copy-start.52 = (f32[4608]{0:T(1024)S(1)}, f32[4608]{0:T(1024)}, u32[]{:S(2)}) copy-start(f32[4608]{0:T(1024)} %get-tuple-element.68) | copy-start | bytes 55300
  864.2 24.4 %copy-start.24 = (f32[24,64]{1,0:T(8,128)S(1)}, f32[24,64]{1,0:T(8,128)}, u32[]{:S(2)}) copy-start(f32[24,64]{1,0:T(8,128)} %get-tuple-element.155) | copy-start | bytes 18436
  865.5 10.1 all-to-all-start.12
  875.6 9.6 all-to-all-start.10
  885.1 11.8 all-to-all-start.8
  897.0 71.9 %all-to-all-start.11 = ((bf16[4,2,98304]{2,1,0:T(2,128)(2,1)}), bf16[4,2,98304]{2,1,0:T(2,128)(2,1)}, u32[]{:S(2)}, u32[]{:S(2)}) async-start(bf16[4,2,98304]{2,1,0:T(2,128)(2,1)} %reshape.422), calls=%async_computation.11 | async-start | bytes 3145728 | tf_op jit(solution)/shard_map/all_to_all | solution.py:71
  985.0 14.1 %copy-start.8 = (bf16[8,160,6,64]{1,3,2,0:T(8,128)(2,1)S(1)}, bf16[8,160,6,64]{1,3,2,0:T(8,128)(2,1)}, u32[]{:S(2)}) copy-start(bf16[8,160,6,64]{1,3,2,0:T(8,128)(2,1)} %copy.181) | copy-start | bytes 2949124
  1313.5 11.8 all-to-all-start.15
  1318.0 12.5 copy-start.57
  1320.2 10.3 copy-start.20
  1320.2 10.3 copy-start.41
  1325.3 24.4 %all-to-all-start.14 = ((bf16[4,2,98304]{2,1,0:T(2,128)(2,1)}), bf16[4,2,98304]{2,1,0:T(2,128)(2,1)}, u32[]{:S(2)}, u32[]{:S(2)}) async-start(bf16[4,2,98304]{2,1,0:T(2,128)(2,1)} %reshape.430), calls=%async_computation.14 | async-start | bytes 3145728 | tf_op jit(solution)/shard_map/all_to_all | solution.py:79
  1368.1 17.2 %copy-start.26 = (f32[8,1536]{1,0:T(8,128)S(1)}, f32[8,1536]{1,0:T(8,128)}, u32[]{:S(2)}) copy-start(f32[8,1536]{1,0:T(8,128)} %get-tuple-element.122) | copy-start | bytes 147460
  1368.1 17.2 %copy-start.54 = (f32[1536]{0:T(1024)S(1)}, f32[1536]{0:T(1024)}, u32[]{:S(2)}) copy-start(f32[1536]{0:T(1024)} %get-tuple-element.75) | copy-start | bytes 18436
  (31 other events, 193.2 us)
Sparse Core Ops, SparseCore 0:
  114.2 69.8 all-gather.6
  186.3 80.7 all-gather.4
  778.6 74.9 all-gather.10
  855.7 73.2 all-gather.8
where the time goes:
time: 1430 us; the launch traced here: 1410 us
  matrix products  482 us (34%)
  other arithmetic  383 us (27%)
  local copies, waits for them, and re-layouts  245 us (17%)
  blocking collectives  203 us (14%)
  starting transfers between devices  48.2 us (3%)
  waiting for transfers between devices  29.6 us (2%)
  between operations  15.4 us (1%)
    sub x16, other arithmetic, sample_attention(): attn_prob = jax.nn.softmax(scores, axis=-1).astype(jnp.bfloat16)  282 us
    dot_general x14, matrix products, linear(): jnp.einsum('bld,de->ble', rows, weight, preferred_element_type=jnp.float32)  152 us
    dot_general x16, matrix products, sample_attention(): jnp.einsum('qhd,khd->hqk', query, keys, preferred_element_type=jnp.float32)  148 us
    dot_general x16, matrix products, sample_attention(): jnp.einsum('hqk,khd->qhd', attn_prob, values, preferred_element_type=jnp....  137 us
    unnamed x166, local copies, waits for them, and re-layouts  86.4 us
    all_to_all x4, blocking collectives, local_blocks(): lax.all_to_all(tensor, 'u', 2, 1, tiled=True)  83.2 us
    all_gather x2, blocking collectives, local_blocks(): lax.all_gather(by_heads[1][1], 'r', axis=1, tiled=True)  70.3 us
    all_to_all x20, local copies, waits for them, and re-layouts, local_blocks(): lax.all_to_all(tensor, 'u', 2, 1, tiled=True)  58 us
  transfers between devices with their start and end apart: 16, of which 5 were waited for; matrix products, arithmetic and copies ran while one was open for 16% of the time, Pallas kernels for 0%

commit v1 on v0

v1 whole, which is shorter than its diff:
```python
import functools
import math

import jax
import jax.numpy as jnp
from jax import lax
from jax.experimental import pallas as pl
from jax.experimental.pallas import tpu as pltpu
from jax.sharding import PartitionSpec as P

EPSILON = 1e-6
MASK_FILL = -1e30
MESH = pl.DeviceIdType.MESH
VMEM = pltpu.VMEM
LANES = 128
TXT_PAD = 48
Q_BLOCK = 256


def place():
    r, u = lax.axis_index('r'), lax.axis_index('u')
    return r, u, r % 2, r // 2


def pick(c, even, odd):
    return (1 - c) * even + c * odd


def remote(src, dst, send, recv, r, u):
    return pltpu.make_async_remote_copy(src_ref=src, dst_ref=dst, send_sem=send, recv_sem=recv, device_id={'r': r, 'u': u}, device_id_type=MESH)


def greet(peers, count):
    barrier = pltpu.get_barrier_semaphore()
    for r, u in peers:
        pl.semaphore_signal(barrier, inc=1, device_id={'r': r, 'u': u}, device_id_type=MESH)
    pl.semaphore_wait(barrier, count)


def scatter_kernel(n, img, txt, mod, img_o, txt_o, mod_o, send, recv, mod_send, mod_recv, local):
    r, u, c, x = place()
    total = 2 * n * n
    me = r * n + u
    others = [(me + d) % total for d in range(1, total)]
    greet([(o // n, o % n) for o in others], total - 1)
    copies = []
    for d, o in enumerate(others):
        ro, uo = o // n, o % n
        sample = pick(ro % 2, uo, n + ro // 2)
        copies.append(remote(mod.at[sample], mod_o.at[me], mod_send.at[d], mod_recv.at[d], ro, uo))
    own_slot = pick(c, u, r)
    targets = []
    for d in list(range(1, n)):
        targets.append((pick(c, r, 2 * ((x + d) % n) + 1), pick(c, (u + d) % n, u), pick(c, (u + d) % n, n + (x + d) % n), own_slot))
    for d in range(n):
        j = (pick(c, x, u) + d) % n
        targets.append((pick(c, 2 * j + 1, 2 * x), pick(c, u, j), pick(c, n + j, j), pick(c, r, n + u)))
    for t, (ro, uo, sample, slot) in enumerate(targets):
        copies.append(remote(img.at[sample], img_o.at[slot], send.at[0, t], recv.at[0, slot], ro, uo))
        copies.append(remote(txt.at[sample], txt_o.at[slot], send.at[1, t], recv.at[1, slot], ro, uo))
    for copy in copies:
        copy.start()
    own_sample = pick(c, u, n + x)
    mine = [
        pltpu.make_async_copy(img.at[own_sample], img_o.at[own_slot], local.at[0]),
        pltpu.make_async_copy(txt.at[own_sample], txt_o.at[own_slot], local.at[1]),
        pltpu.make_async_copy(mod.at[own_sample], mod_o.at[me], local.at[2]),
    ]
    for copy in mine:
        copy.start()
    for copy in copies:
        copy.wait_send()
    for copy in mine:
        copy.wait()
    for d in range(1, total):
        source = (me - d + total) % total
        remote(mod.at[0], mod_o.at[source], mod_send.at[d - 1], mod_recv.at[d - 1], r, u).wait_recv()
    for d in range(1, 2 * n):
        slot = (own_slot + d) % (2 * n)
        remote(img.at[0], img_o.at[slot], send.at[0, 0], recv.at[0, slot], r, u).wait_recv()
        remote(txt.at[0], txt_o.at[slot], send.at[1, 0], recv.at[1, slot], r, u).wait_recv()


def scatter(mesh, img, txt, mod):
    n = mesh.shape['u']
    total = 2 * n * n
    return pl.pallas_call(
        functools.partial(scatter_kernel, n),
        out_shape=[jax.ShapeDtypeStruct(img.shape, img.dtype), jax.ShapeDtypeStruct(txt.shape, txt.dtype), jax.ShapeDtypeStruct((total,) + mod.shape[1:], mod.dtype)],
        in_specs=[pl.BlockSpec(memory_space=VMEM)] * 3,
        out_specs=[pl.BlockSpec(memory_space=VMEM)] * 3,
        scratch_shapes=[pltpu.SemaphoreType.DMA((2, 2 * n)), pltpu.SemaphoreType.DMA((2, 2 * n)), pltpu.SemaphoreType.DMA((total,)), pltpu.SemaphoreType.DMA((total,)), pltpu.SemaphoreType.DMA((3,))],
        compiler_params=pltpu.CompilerParams(collective_id=0, has_side_effects=True),
        name='scatter',
    )(img, txt, mod)


def unscatter_kernel(n, img, txt, img_o, txt_o, send, recv, local):
    r, u, c, x = place()
    own_slot, sample = pick(c, u, r), pick(c, u, n + x)
    senders, targets = [], []
    for d in range(1, 2 * n):
        s = (sample + d) % (2 * n)
        odd = s // n
        senders.append((pick(odd, 2 * x, 2 * (s % n) + 1), pick(odd, s, u)))
        k = (own_slot + d) % (2 * n)
        targets.append((pick(c, 2 * x + k // n, k), pick(c, k % n, u), k))
    greet(senders, 2 * n - 1)
    copies = []
    for t, (ro, uo, k) in enumerate(targets):
        copies.append(remote(img.at[k], img_o.at[sample], send.at[0, t], recv.at[0, sample], ro, uo))
        copies.append(remote(txt.at[k], txt_o.at[sample], send.at[1, t], recv.at[1, sample], ro, uo))
    for copy in copies:
        copy.start()
    mine = [pltpu.make_async_copy(img.at[own_slot], img_o.at[sample], local.at[0]), pltpu.make_async_copy(txt.at[own_slot], txt_o.at[sample], local.at[1])]
    for copy in mine:
        copy.start()
    for copy in copies:
        copy.wait_send()
    for copy in mine:
        copy.wait()
    for d in range(1, 2 * n):
        s = (sample + d) % (2 * n)
        remote(img.at[0], img_o.at[s], send.at[0, 0], recv.at[0, s], r, u).wait_recv()
        remote(txt.at[0], txt_o.at[s], send.at[1, 0], recv.at[1, s], r, u).wait_recv()


def unscatter(mesh, img, txt):
    n = mesh.shape['u']
    return pl.pallas_call(
        functools.partial(unscatter_kernel, n),
        out_shape=[jax.ShapeDtypeStruct(img.shape, img.dtype), jax.ShapeDtypeStruct(txt.shape, txt.dtype)],
        in_specs=[pl.BlockSpec(memory_space=VMEM)] * 2,
        out_specs=[pl.BlockSpec(memory_space=VMEM)] * 2,
        scratch_shapes=[pltpu.SemaphoreType.DMA((2, 2 * n)), pltpu.SemaphoreType.DMA((2, 2 * n)), pltpu.SemaphoreType.DMA((2,))],
        compiler_params=pltpu.CompilerParams(collective_id=1, has_side_effects=True),
        name='unscatter',
    )(img, txt)


def ring_place(n):
    r, u, c, x = place()
    me = pick(c, x, u)

    def peer(d):
        j = (me + d + n) % n
        return pick(c, 2 * j, r), pick(c, u, j)

    return me, peer


def gather_kernel(n, img, txt, img_o, txt_o, send, recv, local):
    me, peer = ring_place(n)
    right, left = peer(1), peer(-1)
    greet([right, left], 2)
    rows = img.shape[0] // 4
    lside, rside, far = (me + n - 1) % n, (me + 1) % n, (me + 2) % n

    def part(ref, txt_ref, q):
        return txt_ref if q == 4 else ref.at[pl.ds(q * rows, rows)]

    def block(slot, q):
        return part(img_o.at[slot], txt_o.at[slot], q)

    copies = []
    for q_right, q_left in zip((0, 1, 4, 2, 3), (2, 3, 4, 0, 1)):
        copies.append(remote(part(img, txt, q_right), block(me, q_right), send.at[0, q_right], recv.at[0, q_right], *right))
        copies.append(remote(part(img, txt, q_left), block(me, q_left), send.at[1, q_left], recv.at[1, q_left], *left))
    for copy in copies:
        copy.start()
    mine = [pltpu.make_async_copy(img, img_o.at[me], local.at[0]), pltpu.make_async_copy(txt, txt_o.at[me], local.at[1])]
    for copy in mine:
        copy.start()

    def arrived(kind, slot, q):
        remote(block(slot, q), block(slot, q), send.at[0, q], recv.at[kind, q], *right).wait_recv()

    for kind, slot, q, target in ((0, lside, 0, right), (1, rside, 2, left), (0, lside, 1, right), (1, rside, 3, left), (0, lside, 4, right)):
        arrived(kind, slot, q)
        copy = remote(block(slot, q), block(slot, q), send.at[2, q], recv.at[2, q], *target)
        copy.start()
        copies.append(copy)
    for kind, slot, parts in ((0, lside, (2, 3)), (1, rside, (4, 0, 1)), (2, far, (0, 2, 1, 3, 4))):
        for q in parts:
            arrived(kind, slot, q)
    for copy in copies:
        copy.wait_send()
    for copy in mine:
        copy.wait()


def gather(mesh, img, txt, collective_id):
    n = mesh.shape['u']
    return pl.pallas_call(
        functools.partial(gather_kernel, n),
        out_shape=[jax.ShapeDtypeStruct((n,) + img.shape, img.dtype), jax.ShapeDtypeStruct((n,) + txt.shape, txt.dtype)],
        in_specs=[pl.BlockSpec(memory_space=VMEM)] * 2,
        out_specs=[pl.BlockSpec(memory_space=VMEM)] * 2,
        scratch_shapes=[pltpu.SemaphoreType.DMA((3, 5)), pltpu.SemaphoreType.DMA((3, 5)), pltpu.SemaphoreType.DMA((2,))],
        compiler_params=pltpu.CompilerParams(collective_id=collective_id, has_side_effects=True),
        name='gather',
    )(img, txt)


def exchange_kernel(n, o, img_o, txt_o, send, recv, local):
    me, peer = ring_place(n)
    greet([peer(d) for d in range(1, n)], n - 1)
    rows, cols = img_o.shape[0], o.shape[1]
    txt_rows = txt_o.shape[0]

    def sources(member):
        return o.at[pl.ds(pl.multiple_of(member * rows, rows), rows)], o.at[pl.ds(pl.multiple_of(n * rows + member * txt_rows, 16), txt_rows)]

    def targets(member):
        span = pl.ds(pl.multiple_of(member * cols, LANES), cols)
        return img_o.at[:, span], txt_o.at[:, span]

    copies = []
    for d in (2, 1, 3):
        for t, (src, dst) in enumerate(zip(sources((me + d) % n), targets(me))):
            copies.append(remote(src, dst, send.at[t, d - 1], recv.at[t, d - 1], *peer(d)))
    for copy in copies:
        copy.start()
    mine = [pltpu.make_async_copy(src, dst, local.at[t]) for t, (src, dst) in enumerate(zip(sources(me), targets(me)))]
    for copy in mine:
        copy.start()
    for copy in copies:
        copy.wait_send()
    for copy in mine:
        copy.wait()
    for d in range(1, n):
        for t, (src, dst) in enumerate(zip(sources(me), targets((me + n - d) % n))):
            remote(src, dst, send.at[t, d - 1], recv.at[t, d - 1], *peer(1)).wait_recv()


def exchange(mesh, o, img_rows, txt_rows, collective_id):
    n = mesh.shape['u']
    return pl.pallas_call(
        functools.partial(exchange_kernel, n),
        out_shape=[jax.ShapeDtypeStruct((img_rows, n * o.shape[1]), o.dtype), jax.ShapeDtypeStruct((txt_rows, n * o.shape[1]), o.dtype)],
        in_specs=[pl.BlockSpec(memory_space=VMEM)],
        out_specs=[pl.BlockSpec(memory_space=VMEM)] * 2,
        scratch_shapes=[pltpu.SemaphoreType.DMA((2, n)), pltpu.SemaphoreType.DMA((2, n)), pltpu.SemaphoreType.DMA((2,))],
        compiler_params=pltpu.CompilerParams(collective_id=collective_id, has_side_effects=True),
        name='exchange',
    )(o)


def attend_kernel(head_dim, me_ref, a_img, a_txt, wq_i, wk_i, wv_i, wq_t, wk_t, wv_t, bias_i, bias_t, gain_i, gain_t, key_bias, o_ref, w_cat, q_s, k_s, v_s):
    img_rows, txt_rows = a_img.shape[0], a_txt.shape[0]
    low = lax.broadcasted_iota(jnp.int32, (Q_BLOCK, LANES), 1) < head_dim

    def unit(part, gain):
        square = part * part
        mask = low[: part.shape[0]]
        first = jnp.sum(jnp.where(mask, square, 0.0), axis=-1, keepdims=True)
        second = jnp.sum(jnp.where(mask, 0.0, square), axis=-1, keepdims=True)
        scale = lax.rsqrt(jnp.where(mask, first, second) * (1.0 / head_dim) + EPSILON)
        return (part * scale * gain).astype(jnp.bfloat16)

    def project(rows, bias, gain, out_rows):
        packed = jnp.dot(rows, w_cat[...], preferred_element_type=jnp.float32) + bias[0]
        q_s[out_rows, :] = unit(packed[:, :LANES], gain[0, :, :LANES])
        k_s[out_rows, :] = unit(packed[:, LANES:2 * LANES], gain[0, :, LANES:])
        v_s[out_rows, :] = packed[:, 2 * LANES:].astype(jnp.bfloat16)

    for t, w in enumerate((wq_t, wk_t, wv_t)):
        w_cat[:, t * LANES:(t + 1) * LANES] = w[0, 0]
    project(a_txt[...], bias_t, gain_t, pl.ds(img_rows, txt_rows))
    tail = pl.ds(img_rows + txt_rows, q_s.shape[0] - img_rows - txt_rows)
    for ref in (q_s, k_s, v_s):
        ref[tail, :] = jnp.zeros((q_s.shape[0] - img_rows - txt_rows, LANES), jnp.bfloat16)
    for t, w in enumerate((wq_i, wk_i, wv_i)):
        w_cat[:, t * LANES:(t + 1) * LANES] = w[0, 0]

    @pl.loop(0, img_rows // Q_BLOCK)
    def _(step):
        span = pl.ds(pl.multiple_of(step * Q_BLOCK, Q_BLOCK), Q_BLOCK)
        project(a_img[span, :], bias_i, gain_i, span)

    factor = math.log2(math.e) / math.sqrt(head_dim)

    @pl.loop(0, q_s.shape[0] // Q_BLOCK)
    def _(step):
        span = pl.ds(pl.multiple_of(step * Q_BLOCK, Q_BLOCK), Q_BLOCK)
        query = q_s[span, :]
        zero = jnp.zeros_like(query)
        keys, values = k_s[...], v_s[...]
        halves = []
        for h in range(2):
            one = jnp.where(low, query, zero) if h == 0 else jnp.where(low, zero, query)
            scores = lax.dot_general(one, keys, (((1,), (1,)), ((), ())), preferred_element_type=jnp.float32)
            scores = jnp.concatenate([scores[:, :img_rows], scores[:, img_rows:] + key_bias[...]], axis=1)
            top = jnp.max(scores, axis=-1, keepdims=True)
            prob = jnp.exp2((scores - top) * factor)
            norm = jnp.sum(prob, axis=-1, keepdims=True)
            halves.append(jnp.dot(prob.astype(jnp.bfloat16), values, preferred_element_type=jnp.float32) / norm)
        o_ref[span, :] = jnp.where(low, halves[0], halves[1]).astype(jnp.bfloat16)


def attend(me, a_img, a_txt, w_qkv, bias, gain, key_bias, block, head_dim):
    n, img_rows, width = a_img.shape
    a_img = a_img.reshape(-1, width)
    a_txt = a_txt.reshape(-1, width)
    rows = a_img.shape[0] + Q_BLOCK
    cols = width // n
    pairs = cols // LANES
    third = width // LANES

    def weight(side, t):
        return pl.BlockSpec((1, 1, width, LANES), lambda p, me_ref: (block, side, 0, t * third + me_ref[0] * pairs + p))

    whole = lambda shape: pl.BlockSpec(shape, lambda p, me_ref: (0,) * len(shape))
    vec = lambda side, size: pl.BlockSpec((1, 1, size), lambda p, me_ref: (side * pairs + p, 0, 0))
    return pl.pallas_call(
        functools.partial(attend_kernel, head_dim),
        out_shape=jax.ShapeDtypeStruct((rows, cols), jnp.bfloat16),
        grid_spec=pltpu.PrefetchScalarGridSpec(
            num_scalar_prefetch=1,
            grid=(pairs,),
            in_specs=[whole(a_img.shape), whole(a_txt.shape)] + [weight(s, t) for s in range(2) for t in range(3)] + [vec(0, 3 * LANES), vec(1, 3 * LANES), vec(0, 2 * LANES), vec(1, 2 * LANES), whole(key_bias.shape)],
            out_specs=pl.BlockSpec((rows, LANES), lambda p, me_ref: (0, p)),
            scratch_shapes=[pltpu.VMEM((width, 3 * LANES), jnp.bfloat16)] + [pltpu.VMEM((rows, LANES), jnp.bfloat16)] * 3,
        ),
        compiler_params=pltpu.CompilerParams(vmem_limit_bytes=60 * 2**20, dimension_semantics=('arbitrary',)),
        cost_estimate=pl.CostEstimate(flops=10**10, bytes_accessed=10**7, transcendentals=0),
        name='attend',
    )(me, a_img, a_txt, w_qkv, w_qkv, w_qkv, w_qkv, w_qkv, w_qkv, bias, bias, gain, gain, key_bias)


def modulated_norm(hidden, shift, scale):
    wide = hidden.astype(jnp.float32)
    centered = wide - jnp.mean(wide, axis=-1, keepdims=True)
    variance = jnp.mean(centered * centered, axis=-1, keepdims=True)
    return ((1.0 + scale) * (centered * lax.rsqrt(variance + EPSILON)) + shift).astype(jnp.bfloat16)


def linear(rows, weight, bias):
    return jnp.dot(rows, weight, preferred_element_type=jnp.float32) + bias.astype(jnp.float32)


def modality_out(hidden, attended, mod, w_proj, b_proj, w_up, b_up, w_down, b_down):
    residual = hidden.astype(jnp.float32) + mod[2] * linear(attended, w_proj, b_proj)
    hidden = residual.astype(jnp.bfloat16)
    normed = modulated_norm(hidden, mod[3], mod[4])
    inner = jax.nn.gelu(linear(normed, w_up, b_up), approximate=True).astype(jnp.bfloat16)
    return (hidden.astype(jnp.float32) + mod[5] * linear(inner, w_down, b_down)).astype(jnp.bfloat16)


def solution(mesh):
    seq_spec = P('dp', ('r', 'u'), None)
    row_spec = P('dp', None)
    n = mesh.shape['u']
    total = n * mesh.shape['r']

    def local_blocks(image, text, cond_vec, key_valid, w_mod, b_mod, w_qkv, b_qkv, q_gain, k_gain, w_proj, b_proj, w_up, b_up, w_down, b_down):
        blocks, _, width, mod_width = w_mod.shape
        heads, head_dim = q_gain.shape[2:]
        r, u = lax.axis_index('r'), lax.axis_index('u')
        c, x = r % 2, r // 2
        sample = jnp.where(c == 0, u, n + x)
        member = jnp.where(c == 0, x, u)
        silu_vec = jax.nn.silu(cond_vec.astype(jnp.float32)).astype(jnp.bfloat16)
        per = blocks * 2 * mod_width // total
        parts = mod_width // per
        me = r * n + u
        which, col = me // parts, (me % parts) * per
        w_mine = lax.dynamic_slice(w_mod, (which // 2, which % 2, 0, col), (1, 1, width, per))[0, 0]
        b_mine = lax.dynamic_slice(b_mod, (which // 2, which % 2, col), (1, 1, per))[0, 0]
        mod_mine = jnp.dot(silu_vec, w_mine, preferred_element_type=jnp.float32) + b_mine.astype(jnp.float32)
        img, txt, mod_all = scatter(mesh, image, text, mod_mine.reshape(-1, per // LANES, LANES))
        mod_all = mod_all.reshape(blocks, 2, 6, 1, width)
        slots, run, _ = img.shape
        txt_run = txt.shape[1]
        img = img.reshape(slots * run, width)
        txt = jnp.pad(txt.reshape(slots * txt_run, width), ((0, TXT_PAD - slots * txt_run), (0, 0)))

        valid = lax.dynamic_slice(key_valid, (sample, 0), (1, key_valid.shape[1]))[0]
        strided = valid.reshape(2 * n, n, txt_run).transpose(1, 0, 2).reshape(-1)
        valid = jnp.where(c == 0, valid, strided).reshape(n, slots * txt_run)
        text_bias = jnp.pad(jnp.where(valid > 0, 0.0, MASK_FILL), ((0, 0), (0, TXT_PAD - slots * txt_run)), constant_values=MASK_FILL).reshape(1, -1)
        key_bias = jnp.pad(text_bias, ((0, 0), (0, Q_BLOCK - n * TXT_PAD)), constant_values=MASK_FILL).astype(jnp.float32)

        pairs = width // n // LANES
        bias_all = b_qkv.astype(jnp.float32).reshape(blocks, 2, 3, n, pairs, LANES)
        bias_all = lax.dynamic_index_in_dim(bias_all, member, 3, keepdims=False).transpose(0, 1, 3, 2, 4).reshape(blocks, 2 * pairs, 1, 3 * LANES)
        gain_all = jnp.stack([q_gain, k_gain], axis=2).astype(jnp.float32).reshape(blocks, 2, 2, n, pairs, LANES)
        gain_all = lax.dynamic_index_in_dim(gain_all, member, 3, keepdims=False).transpose(0, 1, 3, 2, 4).reshape(blocks, 2 * pairs, 1, 2 * LANES)
        member_arr = member.reshape(1).astype(jnp.int32)

        sides = [img, txt]
        for block in range(blocks):
            normed = [modulated_norm(sides[s], mod_all[block, s, 0], mod_all[block, s, 1]) for s in range(2)]
            a_img, a_txt = gather(mesh, normed[0], normed[1], 2 + 2 * block)
            o = attend(member_arr, a_img, a_txt, w_qkv, bias_all[block], gain_all[block], key_bias, block, head_dim)
            attended = exchange(mesh, o, img.shape[0], TXT_PAD, 3 + 2 * block)
            sides = [modality_out(sides[s], attended[s], mod_all[block, s], w_proj[block, s], b_proj[block, s], w_up[block, s], b_up[block, s], w_down[block, s], b_down[block, s]) for s in range(2)]
        img = sides[0].reshape(slots, run, width)
        txt = sides[1][: slots * txt_run].reshape(slots, txt_run, width)
        return unscatter(mesh, img, txt)

    return jax.shard_map(local_blocks, mesh=mesh, in_specs=(seq_spec, seq_spec, row_spec, row_spec) + (P(),) * 12, out_specs=(seq_spec, seq_spec), check_vma=False)
```

time: 1430 us -> 462 us (0.32); the launches traced: 1410 us -> 459 us
  other arithmetic: 383 us -> 13.9 us
  matrix products: 482 us -> 115 us
  Pallas kernels: 0 us -> 314 us
  local copies, waits for them, and re-layouts: 245 us -> 14.3 us
  blocking collectives: 203 us -> 0 us
  starting transfers between devices: 48.2 us -> 0 us
  waiting for transfers between devices: 29.6 us -> 0 us
    dot_general x50 -> x11, matrix products: 482 us -> 115 us  [the longest x10 112 us: linear(): jnp.dot(rows, weight, preferred_element_type=jnp.float32)]
    pallas_call x0 -> x8, Pallas kernels: none -> 314 us  [the longest x2 162 us: attend(): pl.pallas_call(functools.partial(attend_kernel, head_dim), out_shape=jax....]
    sub x16 -> x0, other arithmetic: 282 us -> none  [sample_attention(): attn_prob = jax.nn.softmax(scores, axis=-1).astype(jnp.bfloat16)]
    all_gather x4 -> x0, blocking collectives: 120 us -> none  [the longest x2 70.3 us: local_blocks(): lax.all_gather(by_heads[1][1], 'r', axis=1, tiled=True)]
    all_to_all x4 -> x0, blocking collectives: 83.2 us -> none  [local_blocks(): lax.all_to_all(tensor, 'u', 2, 1, tiled=True)]
    unnamed x166 -> x52, local copies, waits for them, and re-layouts: 86.4 us -> 3.49 us
    concatenate x6 -> x0, other arithmetic: 63.7 us -> none  [the longest x2 28.2 us: local_blocks(): jnp.concatenate([lax.all_gather(by_heads[1][1], 'r', axis=1, tiled=True),...]
    all_to_all x24 -> x0, local copies, waits for them, and re-layouts: 63.6 us -> none  [the longest x20 58 us: local_blocks(): lax.all_to_all(tensor, 'u', 2, 1, tiled=True)]
  transfers between devices with their start and end apart: 16 -> 0, of which waited for: 5 -> 0; matrix products, arithmetic and copies ran while one was open for 16% -> 0% of each run, Pallas kernels for 0% -> 0%
where the time goes in v1:
time: 462 us; the launch traced here: 459 us
  Pallas kernels  314 us (68%)
  matrix products  115 us (25%)
  local copies, waits for them, and re-layouts  14.3 us (3%)
  other arithmetic  13.9 us (3%)
    pallas_call x2, Pallas kernels, attend(): pl.pallas_call(functools.partial(attend_kernel, head_dim), out_shape=jax....  162 us
    dot_general x10, matrix products, linear(): jnp.dot(rows, weight, preferred_element_type=jnp.float32)  112 us
    pallas_call x2, Pallas kernels, gather(): pl.pallas_call(functools.partial(gather_kernel, n), out_shape=[jax.ShapeD...  73.9 us
    pallas_call x2, Pallas kernels, exchange(): pl.pallas_call(functools.partial(exchange_kernel, n), out_shape=[jax.Shap...  31.9 us
    pallas_call x1, Pallas kernels, scatter(): pl.pallas_call(functools.partial(scatter_kernel, n), out_shape=[jax.Shape...  25.9 us
    pallas_call x1, Pallas kernels, unscatter(): pl.pallas_call(functools.partial(unscatter_kernel, n), out_shape=[jax.Sha...  20.4 us

profile of v1, /device:TPU:97, one launch (start us, length us, event | category | flops | bytes accessed | tf_op | source)
XLA Modules:
  0.0 458.7 jit_solution(3491718391102150372)
XLA Ops:
  0.7 0.8 convert_reduce_fusion.13
  1.5 2.6 fusion.244
  4.1 0.7 copy.27.mod
  4.7 0.7 copy.26.txt
  5.5 25.9 %scatter.1 = (bf16[8,64,1536]{2,1,0:T(8,128)(2,1)}, bf16[8,5,1536]{2,1,0:T(8,128)(2,1)}, f32[32,9,128]{2,1,0:T(8,128)}) custom-call(bf16[8,64,1536]{2,1,0:T(8,128)(2,1)} %img.1, bf16[8,5,1536]{2,1,0:T(8,128)(2,1)} %copy.26.txt, f32[8,9,128]{2,1,0:T(8,128)} %copy.27.mod), custom_call_target="tpu_custom_call" | custom-call | tf_op jit(solution)/shard_map/scatter/pallas_call | solution.py:87
  31.4 1.1 reshape.397
  32.9 1.0 reshape.395
  33.9 0.8 fusion.266.txt
  34.7 1.7 convert_reduce_fusion.3
  36.5 0.5 multiply_reduce_fusion
  37.2 1.8 fusion.138.img
  39.0 36.9 %gather.2 = (bf16[4,512,1536]{2,1,0:T(8,128)(2,1)}, bf16[4,48,1536]{2,1,0:T(8,128)(2,1)}) custom-call(bf16[512,1536]{1,0:T(8,128)(2,1)} %fusion.138.img, bf16[48,1536]{1,0:T(8,128)(2,1)} %fusion.266.txt), custom_call_target="tpu_custom_call" | custom-call | tf_op jit(solution)/shard_map/gather/pallas_call | solution.py:194
  75.9 0.5 broadcast.448
  76.5 1.4 fusion.320
  78.2 0.6 pad.14.key_bias
  78.9 0.6 fusion.321
  79.5 0.6 squeeze.46.bias_i.bias_t
  80.4 0.6 fusion.322
  81.0 80.9 %attend.2.o = bf16[2304,384]{1,0:T(8,128)(2,1)} custom-call(s32[1]{0:T(128)} %bitcast.3.me_ref, bf16[2048,1536]{1,0:T(8,128)(2,1)} %bitcast.217, bf16[192,1536]{1,0:T(8,128)(2,1)} %bitcast.220, bf16[2,2,1536,4608]{3,2,1,0:T(8,128)(2,1)} %wv_t.3, bf16[2,2,1536,4608]{3,2,1,0:T(8,128)(2,1)} %wv_t.3, bf16[2,2,1536,4608]{3,2,1,0:T(8,128)(2,1)} %wv_t.3, ...), custom_call_target="tpu_custom_call" | custom-call | flops 10000000000 | bytes 10000000 | tf_op jit(solution)/shard_map/attend/pallas_call | solution.py:315
  161.9 16.0 %exchange.2 = (bf16[512,1536]{1,0:T(8,128)(2,1)}, bf16[48,1536]{1,0:T(8,128)(2,1)}) custom-call(bf16[2304,384]{1,0:T(8,128)(2,1)} %attend.2.o), custom_call_target="tpu_custom_call" | custom-call | tf_op jit(solution)/shard_map/exchange/pallas_call | solution.py:238
  177.9 0.9 slice_reduce_fusion.1
  178.8 0.7 convert_reduce_fusion.6
  179.5 3.5 fusion.327
  182.9 0.2 multiply_reduce_fusion.3
  183.2 0.7 slice_convert_fusion
  183.8 0.7 convert_reduce_fusion.5
  184.5 15.6 %fusion.328 = (f32[48]{0:T(128)S(1)}, f32[48,1536]{1,0:T(8,128)S(1)}) fusion(f32[48,1536]{1,0:T(8,128)S(1)} %get-tuple-element.77, f32[1536]{0:T(1024)S(1)} %get-tuple-element.55, bf16[2,2,6144,1536]{3,2,1,0:T(8,128)(2,1)} %param.30, bf16[2,2,1536,6144]{3,2,1,0:T(8,128)(2,1)} %param.28, f32[6144]{0:T(1024)S(1)} %bitcast.232, ...), kind=kOutput, calls=%fused_computation.295 | convolution fusion | flops 1815699456 | bytes 38692032 | tf_op jit(solution)/shard_map/dot_general | solution.py:339
  200.3 0.8 add_convert_fusion.1.txt
  201.1 5.6 %convert_reduce_fusion.2 = (f32[512]{0:T(512)S(1)}, bf16[512,1536]{1,0:T(8,128)(2,1)S(1)}) fusion(f32[1536]{0:T(1024)S(1)} %get-tuple-element.60, bf16[512,1536]{1,0:T(8,128)(2,1)} %get-tuple-element.18, bf16[2,2,1536,1536]{3,2,1,0:T(8,128)(2,1)} %param.26, f32[1536]{0:T(1024)S(1)} %get-tuple-element.49, bf16[512,1536]{1,0:T(8,128)(2,1)S(1)} %bitcast.216), kind=kOutput, calls=%fused_computation.62 | convolution fusion | flops 2421423616 | bytes 9451520 | tf_op jit(solution)/shard_map/dot_general | solution.py:339
  206.7 0.5 fusion.128
  207.3 16.9 %fusion.31.clone.7.clone.5 = bf16[512,6144]{1,0:T(8,128)(2,1)S(1)} fusion(bf16[2,2,1536,6144]{3,2,1,0:T(8,128)(2,1)} %param.28, f32[6144]{0:T(1024)S(1)} %bitcast.231, bf16[512,1536]{1,0:T(8,128)(2,1)S(1)} %get-tuple-element.73, f32[1536]{0:T(1024)S(1)} %get-tuple-element.46, ...), kind=kOutput, calls=%fused_computation.33.clone.clone.clone.clone.clone.clone.clone.clone.clone.clone... | convolution fusion | flops 9699852288 | bytes 26779648 | tf_op jit(solution)/shard_map/dot_general | solution.py:339
  224.2 14.4 %convert_reduce_fusion.1 = (f32[512]{0:T(512)S(1)}, bf16[512,1536]{1,0:T(8,128)(2,1)S(1)}) fusion(f32[1536]{0:T(1024)S(1)} %get-tuple-element.56, bf16[2,2,6144,1536]{3,2,1,0:T(8,128)(2,1)} %param.30, bf16[512,1536]{1,0:T(8,128)(2,1)S(1)} %get-tuple-element.73, f32[1536]{0:T(1024)S(1)} %get-tuple-element.48, bf16[512,6144]{1,0:T(8,128)(2,1)S(1)} %fusion.31.clone.7.clone.5), kind=kOutput, calls=%fused_computation.59 | convolution fusion | flops 9669181440 | bytes 28325888 | tf_op jit(solution)/shard_map/dot_general | solution.py:339
  238.6 0.5 fusion.124
  239.2 1.8 fusion.127.img
  240.9 36.9 %gather.3 = (bf16[4,512,1536]{2,1,0:T(8,128)(2,1)}, bf16[4,48,1536]{2,1,0:T(8,128)(2,1)}) custom-call(bf16[512,1536]{1,0:T(8,128)(2,1)} %fusion.127.img, bf16[48,1536]{1,0:T(8,128)(2,1)} %add_convert_fusion.1.txt), custom_call_target="tpu_custom_call" | custom-call | tf_op jit(solution)/shard_map/gather/pallas_call | solution.py:194
  277.9 0.6 squeeze.56.bias_i.bias_t
  278.6 81.0 %attend.3.o = bf16[2304,384]{1,0:T(8,128)(2,1)} custom-call(s32[1]{0:T(128)} %bitcast.3.me_ref, bf16[2048,1536]{1,0:T(8,128)(2,1)} %bitcast.218, bf16[192,1536]{1,0:T(8,128)(2,1)} %bitcast.221, bf16[2,2,1536,4608]{3,2,1,0:T(8,128)(2,1)} %wv_t.3, bf16[2,2,1536,4608]{3,2,1,0:T(8,128)(2,1)} %wv_t.3, bf16[2,2,1536,4608]{3,2,1,0:T(8,128)(2,1)} %wv_t.3, ...), custom_call_target="tpu_custom_call" | custom-call | flops 10000000000 | bytes 10000000 | tf_op jit(solution)/shard_map/attend/pallas_call | solution.py:315
  359.5 16.0 %exchange.3 = (bf16[512,1536]{1,0:T(8,128)(2,1)}, bf16[48,1536]{1,0:T(8,128)(2,1)}) custom-call(bf16[2304,384]{1,0:T(8,128)(2,1)} %attend.3.o), custom_call_target="tpu_custom_call" | custom-call | tf_op jit(solution)/shard_map/exchange/pallas_call | solution.py:238
  375.6 3.5 fusion.331
  379.3 15.5 %fusion = f32[48,1536]{1,0:T(8,128)S(1)} fusion(bf16[2,2,6144,1536]{3,2,1,0:T(8,128)(2,1)} %param.30, bf16[2,2,1536,6144]{3,2,1,0:T(8,128)(2,1)} %param.28, f32[6144]{0:T(1024)S(1)} %bitcast.230, f32[48,1536]{1,0:T(8,128)S(1)} %get-tuple-element.83, f32[1536]{0:T(1024)S(1)} %copy-done.21, f32[48]{0:T(128)S(1)} %add_rsqrt_fusion.4, ...), kind=kOutput, calls=%fused_computation.2 | convolution fusion | flops 1815257088 | bytes 38375808 | tf_op jit(solution)/shard_map/dot_general | solution.py:339
  394.9 0.7 reshape.407.txt
  395.6 5.6 %convert_reduce_fusion = (f32[512]{0:T(512)S(1)}, bf16[512,1536]{1,0:T(8,128)(2,1)S(1)}) fusion(f32[1536]{0:T(1024)S(1)} %copy-done.19, bf16[512,1536]{1,0:T(8,128)(2,1)} %get-tuple-element.22, bf16[2,2,1536,1536]{3,2,1,0:T(8,128)(2,1)} %param.26, f32[1536]{0:T(1024)S(1)} %copy-done.18, bf16[512,1536]{1,0:T(8,128)(2,1)S(1)} %get-tuple-element.75), kind=kOutput, calls=%fused_computation.56 | convolution fusion | flops 2421423616 | bytes 9451520 | tf_op jit(solution)/shard_map/dot_general | solution.py:339
  401.3 0.6 fusion.120
  401.9 17.2 %fusion.39.clone.11 = bf16[512,6144]{1,0:T(8,128)(2,1)S(1)} fusion(bf16[2,2,1536,6144]{3,2,1,0:T(8,128)(2,1)} %param.28, f32[6144]{0:T(1024)S(1)} %bitcast.229, bf16[512,1536]{1,0:T(8,128)(2,1)S(1)} %get-tuple-element.81, f32[1536]{0:T(1024)S(1)} %copy-done.16, f32[512]{0:T(512)S(1)} %add_rsqrt_fusion.1, ...), kind=kOutput, calls=%fused_computation.41.clone.clone.clone.clone.clone.clone.clone.clone.clone.2 | convolution fusion | flops 9699852288 | bytes 26779648 | tf_op jit(solution)/shard_map/dot_general | solution.py:339
  419.0 14.8 %fusion.134 = bf16[512,1536]{1,0:T(8,128)(2,1)} fusion(bf16[512,1536]{1,0:T(8,128)(2,1)S(1)} %get-tuple-element.81, bf16[2,2,6144,1536]{3,2,1,0:T(8,128)(2,1)} %param.30, f32[1536]{0:T(1024)S(1)} %copy-done.20, f32[1536]{0:T(1024)S(1)} %copy-done.15, bf16[512,6144]{1,0:T(8,128)(2,1)S(1)} %fusion.39.clone.11), kind=kOutput, calls=%fused_computation.107 | convolution fusion | flops 9667608576 | bytes 28323840 | tf_op jit(solution)/shard_map/dot_general | solution.py:339
  433.8 20.4 %unscatter.1 = (bf16[8,64,1536]{2,1,0:T(8,128)(2,1)}, bf16[8,5,1536]{2,1,0:T(8,128)(2,1)}) custom-call(bf16[8,64,1536]{2,1,0:T(8,128)(2,1)} %bitcast.219, bf16[8,5,1536]{2,1,0:T(8,128)(2,1)} %reshape.407.txt), custom_call_target="tpu_custom_call" | custom-call | tf_op jit(solution)/shard_map/unscatter/pallas_call | solution.py:130
  454.2 1.6 copy.33
  455.8 2.7 copy.39
  (90 shorter events, 1.9 us)
Async XLA Ops:
  0.6 4.1 copy-start.4
  31.4 5.0 %copy-start = (bf16[8,64,1536]{2,1,0:T(8,128)(2,1)S(1)}, bf16[8,64,1536]{2,1,0:T(8,128)(2,1)}, u32[]{:S(2)}) copy-start(bf16[8,64,1536]{2,1,0:T(8,128)(2,1)} %get-tuple-element.13) | copy-start | bytes 4718596
  36.4 42.4 %copy-start.7 = (bf16[2,2,4608]{2,1,0:T(2,128)(2,1)S(1)}, bf16[2,2,4608]{2,1,0:T(2,128)(2,1)}, u32[]{:S(2)}) copy-start(bf16[2,2,4608]{2,1,0:T(2,128)(2,1)} %param.23) | copy-start | bytes 110596
  36.4 43.7 %copy-start.13 = (bf16[2,2,24,64]{3,2,1,0:T(8,128)(2,1)S(1)}, bf16[2,2,24,64]{3,2,1,0:T(8,128)(2,1)}, u32[]{:S(2)}) copy-start(bf16[2,2,24,64]{3,2,1,0:T(8,128)(2,1)} %param.25) | copy-start | bytes 36868
  36.4 43.8 %copy-start.14 = (bf16[2,2,24,64]{3,2,1,0:T(8,128)(2,1)S(1)}, bf16[2,2,24,64]{3,2,1,0:T(8,128)(2,1)}, u32[]{:S(2)}) copy-start(bf16[2,2,24,64]{3,2,1,0:T(8,128)(2,1)} %param.24) | copy-start | bytes 36868
  81.0 97.8 %copy-start.5 = (bf16[2,2,1536]{2,1,0:T(2,128)(2,1)S(1)}, bf16[2,2,1536]{2,1,0:T(2,128)(2,1)}, u32[]{:S(2)}) copy-start(bf16[2,2,1536]{2,1,0:T(2,128)(2,1)} %param.27) | copy-start | bytes 36868
  177.9 5.2 %copy-start.3 = (bf16[2,2,6144]{2,1,0:T(2,128)(2,1)S(1)}, bf16[2,2,6144]{2,1,0:T(2,128)(2,1)}, u32[]{:S(2)}) copy-start(bf16[2,2,6144]{2,1,0:T(2,128)(2,1)} %param.29) | copy-start | bytes 147460
  178.8 5.1 %copy-start.6 = (bf16[2,2,1536]{2,1,0:T(2,128)(2,1)S(1)}, bf16[2,2,1536]{2,1,0:T(2,128)(2,1)}, u32[]{:S(2)}) copy-start(bf16[2,2,1536]{2,1,0:T(2,128)(2,1)} %param.31) | copy-start | bytes 36868
  200.1 6.6 %copy-start.1 = (f32[48,1536]{1,0:T(8,128)}, f32[48,1536]{1,0:T(8,128)S(1)}, u32[]{:S(2)}) copy-start(f32[48,1536]{1,0:T(8,128)S(1)} %get-tuple-element.79) | copy-start | bytes 884740
  238.6 39.3 %copy-start.8 = (f32[1,2,3,3,128]{4,1,2,3,0:T(2,128)S(1)}, f32[1,2,3,3,128]{4,1,2,3,0:T(2,128)}, u32[]{:S(2)}) copy-start(f32[1,2,3,3,128]{4,1,2,3,0:T(2,128)} %get-tuple-element.68) | copy-start | bytes 27652
  278.5 97.0 %copy-start.2 = (f32[48,1536]{1,0:T(8,128)S(1)}, f32[48,1536]{1,0:T(8,128)}, u32[]{:S(2)}) copy-start(f32[48,1536]{1,0:T(8,128)} %copy-done.1) | copy-start | bytes 884740
  278.5 97.0 %copy-start.23 = (f32[1536]{0:T(1024)S(1)}, f32[1536]{0:T(1024)}, u32[]{:S(2)}) copy-start(f32[1536]{0:T(1024)} %get-tuple-element.33) | copy-start | bytes 18436
  278.5 97.0 %copy-start.24 = (f32[1536]{0:T(1024)S(1)}, f32[1536]{0:T(1024)}, u32[]{:S(2)}) copy-start(f32[1536]{0:T(1024)} %get-tuple-element.58) | copy-start | bytes 18436
  375.5 3.8 copy-start.12
  375.5 3.8 copy-start.21
  375.5 3.8 copy-start.22
  379.3 15.5 %copy-start.9 = (f32[1536]{0:T(1024)S(1)}, f32[1536]{0:T(1024)}, u32[]{:S(2)}) copy-start(f32[1536]{0:T(1024)} %get-tuple-element.30) | copy-start | bytes 18436
  379.3 15.5 %copy-start.10 = (f32[1536]{0:T(1024)S(1)}, f32[1536]{0:T(1024)}, u32[]{:S(2)}) copy-start(f32[1536]{0:T(1024)} %get-tuple-element.54) | copy-start | bytes 18436
  379.3 16.3 %copy-start.18 = (f32[1536]{0:T(1024)S(1)}, f32[1536]{0:T(1024)}, u32[]{:S(2)}) copy-start(f32[1536]{0:T(1024)} %get-tuple-element.45) | copy-start | bytes 18436
  379.3 16.3 %copy-start.19 = (f32[1536]{0:T(1024)S(1)}, f32[1536]{0:T(1024)}, u32[]{:S(2)}) copy-start(f32[1536]{0:T(1024)} %get-tuple-element.61) | copy-start | bytes 18436
  395.6 6.2 %copy-start.11 = (f32[1,1,6144]{2,1,0:T(1,128)S(1)}, f32[1,1,6144]{2,1,0:T(1,128)}, u32[]{:S(2)}) copy-start(f32[1,1,6144]{2,1,0:T(1,128)} %get-tuple-element.67) | copy-start | bytes 73732
  395.6 6.2 %copy-start.16 = (f32[1536]{0:T(1024)S(1)}, f32[1536]{0:T(1024)}, u32[]{:S(2)}) copy-start(f32[1536]{0:T(1024)} %get-tuple-element.34) | copy-start | bytes 18436
  395.6 6.2 %copy-start.17 = (f32[1536]{0:T(1024)S(1)}, f32[1536]{0:T(1024)}, u32[]{:S(2)}) copy-start(f32[1536]{0:T(1024)} %get-tuple-element.35) | copy-start | bytes 18436
  401.9 17.2 %copy-start.15 = (f32[1536]{0:T(1024)S(1)}, f32[1536]{0:T(1024)}, u32[]{:S(2)}) copy-start(f32[1536]{0:T(1024)} %get-tuple-element.36) | copy-start | bytes 18436
  401.9 17.2 %copy-start.20 = (f32[1536]{0:T(1024)S(1)}, f32[1536]{0:T(1024)}, u32[]{:S(2)}) copy-start(f32[1536]{0:T(1024)} %get-tuple-element.57) | copy-start | bytes 18436

commit v2 on v1

v2 whole, which is shorter than its diff:
```python
import functools
import math

import jax
import jax.numpy as jnp
from jax import lax
from jax.experimental import pallas as pl
from jax.experimental.pallas import tpu as pltpu
from jax.sharding import PartitionSpec as P

EPSILON = 1e-6
MASK_FILL = -1e30
MESH = pl.DeviceIdType.MESH
VMEM = pltpu.VMEM
LANES = 128
TXT_PAD = 48
TXT_ROWS = 256
Q_BLOCK = 768
K_BLOCK = 256


def place():
    r, u = lax.axis_index('r'), lax.axis_index('u')
    return r, u, r % 2, r // 2


def pick(c, even, odd):
    return (1 - c) * even + c * odd


def remote(src, dst, send, recv, r, u):
    return pltpu.make_async_remote_copy(src_ref=src, dst_ref=dst, send_sem=send, recv_sem=recv, device_id={'r': r, 'u': u}, device_id_type=MESH)


def greet(peers, count):
    barrier = pltpu.get_barrier_semaphore()
    for r, u in peers:
        pl.semaphore_signal(barrier, inc=1, device_id={'r': r, 'u': u}, device_id_type=MESH)
    pl.semaphore_wait(barrier, count)


def scatter_kernel(n, img, txt, mod, img_o, txt_o, mod_o, send, recv, mod_send, mod_recv, local):
    r, u, c, x = place()
    total = 2 * n * n
    me = r * n + u
    others = [(me + d) % total for d in range(1, total)]
    greet([(o // n, o % n) for o in others], total - 1)
    copies = []
    for d, o in enumerate(others):
        ro, uo = o // n, o % n
        sample = pick(ro % 2, uo, n + ro // 2)
        copies.append(remote(mod.at[sample], mod_o.at[me], mod_send.at[d], mod_recv.at[d], ro, uo))
    own_slot = pick(c, u, r)
    targets = []
    for d in list(range(1, n)):
        targets.append((pick(c, r, 2 * ((x + d) % n) + 1), pick(c, (u + d) % n, u), pick(c, (u + d) % n, n + (x + d) % n), own_slot))
    for d in range(n):
        j = (pick(c, x, u) + d) % n
        targets.append((pick(c, 2 * j + 1, 2 * x), pick(c, u, j), pick(c, n + j, j), pick(c, r, n + u)))
    for t, (ro, uo, sample, slot) in enumerate(targets):
        copies.append(remote(img.at[sample], img_o.at[slot], send.at[0, t], recv.at[0, slot], ro, uo))
        copies.append(remote(txt.at[sample], txt_o.at[slot], send.at[1, t], recv.at[1, slot], ro, uo))
    for copy in copies:
        copy.start()
    own_sample = pick(c, u, n + x)
    mine = [
        pltpu.make_async_copy(img.at[own_sample], img_o.at[own_slot], local.at[0]),
        pltpu.make_async_copy(txt.at[own_sample], txt_o.at[own_slot], local.at[1]),
        pltpu.make_async_copy(mod.at[own_sample], mod_o.at[me], local.at[2]),
    ]
    for copy in mine:
        copy.start()
    for copy in copies:
        copy.wait_send()
    for copy in mine:
        copy.wait()
    for d in range(1, total):
        source = (me - d + total) % total
        remote(mod.at[0], mod_o.at[source], mod_send.at[d - 1], mod_recv.at[d - 1], r, u).wait_recv()
    for d in range(1, 2 * n):
        slot = (own_slot + d) % (2 * n)
        remote(img.at[0], img_o.at[slot], send.at[0, 0], recv.at[0, slot], r, u).wait_recv()
        remote(txt.at[0], txt_o.at[slot], send.at[1, 0], recv.at[1, slot], r, u).wait_recv()


def scatter(mesh, img, txt, mod):
    n = mesh.shape['u']
    total = 2 * n * n
    return pl.pallas_call(
        functools.partial(scatter_kernel, n),
        out_shape=[jax.ShapeDtypeStruct(img.shape, img.dtype), jax.ShapeDtypeStruct(txt.shape, txt.dtype), jax.ShapeDtypeStruct((total,) + mod.shape[1:], mod.dtype)],
        in_specs=[pl.BlockSpec(memory_space=VMEM)] * 3,
        out_specs=[pl.BlockSpec(memory_space=VMEM)] * 3,
        scratch_shapes=[pltpu.SemaphoreType.DMA((2, 2 * n)), pltpu.SemaphoreType.DMA((2, 2 * n)), pltpu.SemaphoreType.DMA((total,)), pltpu.SemaphoreType.DMA((total,)), pltpu.SemaphoreType.DMA((3,))],
        compiler_params=pltpu.CompilerParams(collective_id=0, has_side_effects=True),
        name='scatter',
    )(img, txt, mod)


def unscatter_kernel(n, img, txt, img_o, txt_o, send, recv, local):
    r, u, c, x = place()
    own_slot, sample = pick(c, u, r), pick(c, u, n + x)
    senders, targets = [], []
    for d in range(1, 2 * n):
        s = (sample + d) % (2 * n)
        odd = s // n
        senders.append((pick(odd, 2 * x, 2 * (s % n) + 1), pick(odd, s, u)))
        k = (own_slot + d) % (2 * n)
        targets.append((pick(c, 2 * x + k // n, k), pick(c, k % n, u), k))
    greet(senders, 2 * n - 1)
    copies = []
    for t, (ro, uo, k) in enumerate(targets):
        copies.append(remote(img.at[k], img_o.at[sample], send.at[0, t], recv.at[0, sample], ro, uo))
        copies.append(remote(txt.at[k], txt_o.at[sample], send.at[1, t], recv.at[1, sample], ro, uo))
    for copy in copies:
        copy.start()
    mine = [pltpu.make_async_copy(img.at[own_slot], img_o.at[sample], local.at[0]), pltpu.make_async_copy(txt.at[own_slot], txt_o.at[sample], local.at[1])]
    for copy in mine:
        copy.start()
    for copy in copies:
        copy.wait_send()
    for copy in mine:
        copy.wait()
    for d in range(1, 2 * n):
        s = (sample + d) % (2 * n)
        remote(img.at[0], img_o.at[s], send.at[0, 0], recv.at[0, s], r, u).wait_recv()
        remote(txt.at[0], txt_o.at[s], send.at[1, 0], recv.at[1, s], r, u).wait_recv()


def unscatter(mesh, img, txt):
    n = mesh.shape['u']
    return pl.pallas_call(
        functools.partial(unscatter_kernel, n),
        out_shape=[jax.ShapeDtypeStruct(img.shape, img.dtype), jax.ShapeDtypeStruct(txt.shape, txt.dtype)],
        in_specs=[pl.BlockSpec(memory_space=VMEM)] * 2,
        out_specs=[pl.BlockSpec(memory_space=VMEM)] * 2,
        scratch_shapes=[pltpu.SemaphoreType.DMA((2, 2 * n)), pltpu.SemaphoreType.DMA((2, 2 * n)), pltpu.SemaphoreType.DMA((2,))],
        compiler_params=pltpu.CompilerParams(collective_id=1, has_side_effects=True),
        name='unscatter',
    )(img, txt)


def ring_place(n):
    r, u, c, x = place()
    me = pick(c, x, u)

    def peer(d):
        j = (me + d + n) % n
        return pick(c, 2 * j, r), pick(c, u, j)

    return me, peer


def joint_kernel(n, head_dim, block, img, txt, w_qkv, bias, gain, key_bias, img_o, txt_o, a_img, a_txt, w_i, w_t, q_s, k_s, v_s, s_a, s_b, o_s, send, recv, o_send, o_recv, local):
    me, peer = ring_place(n)
    right, left = peer(1), peer(-1)
    rows, width = img.shape
    txt_rows = txt.shape[0]
    img_rows = n * rows
    pairs, all_rows = q_s.shape[:2]
    cols = pairs * LANES
    weights = []
    for side, ref in ((0, w_i), (1, w_t)):
        for t in range(3):
            start = pl.multiple_of(t * width + me * cols, LANES)
            weights.append(pltpu.make_async_copy(w_qkv.at[block, side, :, pl.ds(start, cols)], ref.at[:, pl.ds(t * cols, cols)], local.at[2 + 3 * side + t]))
    for copy in weights:
        copy.start()
    mine = [pltpu.make_async_copy(img, a_img.at[me], local.at[0]), pltpu.make_async_copy(txt, a_txt.at[me], local.at[1])]
    for copy in mine:
        copy.start()
    greet([peer(d) for d in range(1, n)], n - 1)
    piece = rows // 4
    lside, rside, far = (me + n - 1) % n, (me + 1) % n, (me + 2) % n

    def part(ref, txt_ref, q):
        return txt_ref if q == 4 else ref.at[pl.ds(q * piece, piece)]

    def landing(slot, q):
        return part(a_img.at[slot], a_txt.at[slot], q)

    copies = []
    for q_right, q_left in zip((0, 1, 4, 2, 3), (2, 3, 4, 0, 1)):
        copies.append(remote(part(img, txt, q_right), landing(me, q_right), send.at[0, q_right], recv.at[0, q_right], *right))
        copies.append(remote(part(img, txt, q_left), landing(me, q_left), send.at[1, q_left], recv.at[1, q_left], *left))
    for copy in copies:
        copy.start()

    def arrived(kind, slot, q):
        remote(landing(slot, q), landing(slot, q), send.at[0, q], recv.at[kind, q], *right).wait_recv()

    def forward(kind, slot, q, target):
        arrived(kind, slot, q)
        copy = remote(landing(slot, q), landing(slot, q), send.at[2, q], recv.at[2, q], *target)
        copy.start()

    low = lax.broadcasted_iota(jnp.int32, (Q_BLOCK, LANES), 1) < head_dim

    def unit(part, scale_by):
        square = part * part
        mask = low[: part.shape[0]]
        first = jnp.sum(jnp.where(mask, square, 0.0), axis=-1, keepdims=True)
        second = jnp.sum(jnp.where(mask, 0.0, square), axis=-1, keepdims=True)
        scale = lax.rsqrt(jnp.where(mask, first, second) * (1.0 / head_dim) + EPSILON)
        return (part * scale * scale_by).astype(jnp.bfloat16)

    def project(tokens, weight, side, spans):
        for tile in range(0, 3 * pairs, 2):
            count = min(2, 3 * pairs - tile)
            lanes = slice(tile * LANES, (tile + count) * LANES)
            packed = jnp.dot(tokens, weight[:, lanes], preferred_element_type=jnp.float32) + bias[side:side + 1, lanes]
            for k in range(count):
                kind, p = (tile + k) // pairs, (tile + k) % pairs
                value = packed[:, k * LANES:(k + 1) * LANES]
                if kind < 2:
                    value = unit(value, gain[side:side + 1, (tile + k) * LANES:(tile + k + 1) * LANES])
                else:
                    value = value.T.astype(jnp.bfloat16)
                offset = 0
                for start, size in spans:
                    if kind == 0:
                        q_s[p, pl.ds(start, size), :] = value[offset:offset + size]
                    elif kind == 1:
                        k_s[p, pl.ds(start, size), :] = value[offset:offset + size]
                    else:
                        v_s[p, :, pl.ds(start, size)] = value[:, offset:offset + size]
                    offset += size

    for copy in weights + mine:
        copy.wait()
    half_rows = rows // 2

    @pl.loop(0, n)
    def _(step):
        @pl.when(step == 1)
        def _():
            forward(0, lside, 0, right)
            forward(1, rside, 2, left)
            forward(0, lside, 4, right)
            forward(0, lside, 1, right)
            forward(1, rside, 3, left)

        @pl.when(step == 2)
        def _():
            for q in (2, 3):
                arrived(0, lside, q)
            for q in (4, 0, 1):
                arrived(1, rside, q)

        @pl.when(step == 3)
        def _():
            for q in (4, 0, 2, 1, 3):
                arrived(2, far, q)

        shift = (3 * step + 3 * (step // 2) + 2 * (step // 3)) % n
        one, two = (me + shift) % n, (me + n - shift) % n
        tokens = jnp.concatenate([a_img[one, :half_rows, :], a_img[two, half_rows:, :]], axis=0)
        project(tokens, w_i, 0, ((pl.multiple_of(one * rows, half_rows), half_rows), (pl.multiple_of(two * rows + half_rows, half_rows), half_rows)))

    fill = jnp.zeros((all_rows - img_rows - n * txt_rows, width), txt.dtype)
    project(jnp.concatenate([a_txt[...].reshape(n * txt_rows, width), fill], axis=0), w_t, 1, ((img_rows, all_rows - img_rows),))

    factor = math.log2(math.e) / math.sqrt(head_dim)
    chunks = all_rows // K_BLOCK
    blocks = all_rows // Q_BLOCK

    def query(index, h):
        value = q_s[index // blocks, pl.ds(pl.multiple_of((index % blocks) * Q_BLOCK, Q_BLOCK), Q_BLOCK), :]
        zero = jnp.zeros_like(value)
        return jnp.where(low, value, zero) if h == 0 else jnp.where(low, zero, value)

    def fold(tile):
        return tile.reshape(tile.shape[0] // 8, 8, tile.shape[1])

    def score(index, value, s_ref, ch, top):
        span = slice(ch * K_BLOCK, (ch + 1) * K_BLOCK)
        tile = lax.dot_general(k_s[index // blocks, span, :], value, (((1,), (1,)), ((), ())), preferred_element_type=jnp.float32)
        if ch == chunks - 1:
            tile = tile + jnp.concatenate([key_bias[...]] * (Q_BLOCK // LANES), axis=1)
        s_ref[span, :] = tile
        peak = jnp.max(fold(tile), axis=0)
        return peak if top is None else jnp.maximum(top, peak)

    def weigh(index, h, s_ref, ch, top, norm, out):
        span = slice(ch * K_BLOCK, (ch + 1) * K_BLOCK)
        prob = jnp.exp2((s_ref[span, :] - top) * factor)
        norm = norm + jnp.sum(fold(prob), axis=0)
        out = out + jnp.dot(v_s[index // blocks, h * head_dim:(h + 1) * head_dim, span], prob.astype(jnp.bfloat16), preferred_element_type=jnp.float32)
        return norm, out

    def stage(next_index, next_h, s_next, index, h, s_now, top_now):
        top = None
        value = query(next_index, next_h)
        norm = jnp.zeros((8, Q_BLOCK), jnp.float32)
        out = jnp.zeros((head_dim, Q_BLOCK), jnp.float32)
        for ch in range(chunks):
            top = score(next_index, value, s_next, ch, top)
            norm, out = weigh(index, h, s_now, ch, top_now, norm, out)
        return jnp.max(top, axis=0, keepdims=True), out / jnp.sum(norm, axis=0, keepdims=True)

    def o_copies(p, d, owner):
        member = (me + d) % n
        lanes = pl.ds(pl.multiple_of(owner * cols + p * LANES, LANES), LANES)
        sources = (o_s.at[p, pl.ds(pl.multiple_of(member * rows, rows), rows)], o_s.at[p, pl.ds(pl.multiple_of(img_rows + member * txt_rows, 16), txt_rows)])
        return list(zip(sources, (img_o.at[:, lanes], txt_o.at[:, lanes])))

    def o_remote(p, d, owner):
        return [remote(src, dst, o_send.at[p, d, t], o_recv.at[p, d, t], *peer(d)) for t, (src, dst) in enumerate(o_copies(p, d, owner))]

    top = None
    value = query(0, 0)
    for ch in range(chunks):
        top = score(0, value, s_a, ch, top)
    top = jnp.max(top, axis=0, keepdims=True)
    steps = pairs * blocks

    def body(step, top_a):
        after = (step + 1) % steps
        top_b, out_a = stage(step, 1, s_b, step, 0, s_a, top_a)
        top_a, out_b = stage(after, 0, s_a, step, 1, s_b, top_b)
        p, b = step // blocks, step % blocks
        o_s[p, pl.ds(pl.multiple_of(b * Q_BLOCK, Q_BLOCK), Q_BLOCK), :] = jnp.concatenate([out_a, out_b], axis=0).T.astype(jnp.bfloat16)

        @pl.when(b == blocks - 1)
        def _():
            for d in (2, 1, 3):
                for copy in o_remote(p, d, me):
                    copy.start()
            for t, (src, dst) in enumerate(o_copies(p, 0, me)):
                pltpu.make_async_copy(src, dst, o_send.at[p, 0, t]).start()

        return top_a

    lax.fori_loop(0, steps, body, top)
    for copy in copies:
        copy.wait_send()
    for kind, slot, q, target in ((0, lside, 0, right), (1, rside, 2, left), (0, lside, 1, right), (1, rside, 3, left), (0, lside, 4, right)):
        remote(landing(slot, q), landing(slot, q), send.at[2, q], recv.at[2, q], *target).wait_send()
    for p in range(pairs):
        for t, (src, dst) in enumerate(o_copies(p, 0, me)):
            pltpu.make_async_copy(src, dst, o_send.at[p, 0, t]).wait()
        for d in range(1, n):
            for copy in o_remote(p, d, me):
                copy.wait_send()
            for copy in o_remote(p, d, (me + n - d) % n):
                copy.wait_recv()


def joint(mesh, img, txt, w_qkv, bias, gain, key_bias, block, head_dim, collective_id):
    n = mesh.shape['u']
    width = img.shape[1]
    all_rows = n * img.shape[0] + TXT_ROWS
    cols = width // n
    pairs = cols // LANES
    bf16, f32 = jnp.bfloat16, jnp.float32
    vmem = pl.BlockSpec(memory_space=VMEM)
    return pl.pallas_call(
        functools.partial(joint_kernel, n, head_dim, block),
        out_shape=[jax.ShapeDtypeStruct(img.shape, bf16), jax.ShapeDtypeStruct(txt.shape, bf16)],
        in_specs=[vmem, vmem, pl.BlockSpec(memory_space=pl.ANY), vmem, vmem, vmem],
        out_specs=[vmem, vmem],
        scratch_shapes=[
            pltpu.VMEM((n,) + img.shape, bf16), pltpu.VMEM((n,) + txt.shape, bf16),
            pltpu.VMEM((width, 3 * cols), bf16), pltpu.VMEM((width, 3 * cols), bf16),
            pltpu.VMEM((pairs, all_rows, LANES), bf16), pltpu.VMEM((pairs, all_rows, LANES), bf16), pltpu.VMEM((pairs, LANES, all_rows), bf16),
            pltpu.VMEM((all_rows, Q_BLOCK), f32), pltpu.VMEM((all_rows, Q_BLOCK), f32),
            pltpu.VMEM((pairs, all_rows, LANES), bf16),
            pltpu.SemaphoreType.DMA((3, 5)), pltpu.SemaphoreType.DMA((3, 5)),
            pltpu.SemaphoreType.DMA((pairs, n, 2)), pltpu.SemaphoreType.DMA((pairs, n, 2)),
            pltpu.SemaphoreType.DMA((8,)),
        ],
        compiler_params=pltpu.CompilerParams(collective_id=collective_id, has_side_effects=True, vmem_limit_bytes=60 * 2**20),
        cost_estimate=pl.CostEstimate(flops=4 * 10**10, bytes_accessed=10**7, transcendentals=0),
        name='joint',
    )(img, txt, w_qkv, bias, gain, key_bias)


def modulated_norm(hidden, shift, scale):
    wide = hidden.astype(jnp.float32)
    centered = wide - jnp.mean(wide, axis=-1, keepdims=True)
    variance = jnp.mean(centered * centered, axis=-1, keepdims=True)
    return ((1.0 + scale) * (centered * lax.rsqrt(variance + EPSILON)) + shift).astype(jnp.bfloat16)


def linear(rows, weight, bias):
    return jnp.dot(rows, weight, preferred_element_type=jnp.float32) + bias.astype(jnp.float32)


def modality_out(hidden, attended, mod, w_proj, b_proj, w_up, b_up, w_down, b_down):
    residual = hidden.astype(jnp.float32) + mod[2] * linear(attended, w_proj, b_proj)
    hidden = residual.astype(jnp.bfloat16)
    normed = modulated_norm(hidden, mod[3], mod[4])
    inner = jax.nn.gelu(linear(normed, w_up, b_up), approximate=True).astype(jnp.bfloat16)
    return (hidden.astype(jnp.float32) + mod[5] * linear(inner, w_down, b_down)).astype(jnp.bfloat16)


def solution(mesh):
    seq_spec = P('dp', ('r', 'u'), None)
    row_spec = P('dp', None)
    n = mesh.shape['u']
    total = n * mesh.shape['r']

    def local_blocks(image, text, cond_vec, key_valid, w_mod, b_mod, w_qkv, b_qkv, q_gain, k_gain, w_proj, b_proj, w_up, b_up, w_down, b_down):
        blocks, _, width, mod_width = w_mod.shape
        heads, head_dim = q_gain.shape[2:]
        r, u = lax.axis_index('r'), lax.axis_index('u')
        c, x = r % 2, r // 2
        sample = jnp.where(c == 0, u, n + x)
        member = jnp.where(c == 0, x, u)
        silu_vec = jax.nn.silu(cond_vec.astype(jnp.float32)).astype(jnp.bfloat16)
        per = blocks * 2 * mod_width // total
        parts = mod_width // per
        me = r * n + u
        which, col = me // parts, (me % parts) * per
        w_mine = lax.dynamic_slice(w_mod, (which // 2, which % 2, 0, col), (1, 1, width, per))[0, 0]
        b_mine = lax.dynamic_slice(b_mod, (which // 2, which % 2, col), (1, 1, per))[0, 0]
        mod_mine = jnp.dot(silu_vec, w_mine, preferred_element_type=jnp.float32) + b_mine.astype(jnp.float32)
        img, txt, mod_all = scatter(mesh, image, text, mod_mine.reshape(-1, per // LANES, LANES))
        mod_all = mod_all.reshape(blocks, 2, 6, 1, width)
        slots, run, _ = img.shape
        txt_run = txt.shape[1]
        img = img.reshape(slots * run, width)
        txt = jnp.pad(txt.reshape(slots * txt_run, width), ((0, TXT_PAD - slots * txt_run), (0, 0)))

        valid = lax.dynamic_slice(key_valid, (sample, 0), (1, key_valid.shape[1]))[0]
        strided = valid.reshape(2 * n, n, txt_run).transpose(1, 0, 2).reshape(-1)
        valid = jnp.where(c == 0, valid, strided).reshape(n, slots * txt_run)
        text_bias = jnp.pad(jnp.where(valid > 0, 0.0, MASK_FILL), ((0, 0), (0, TXT_PAD - slots * txt_run)), constant_values=MASK_FILL).reshape(1, -1)
        text_bias = jnp.pad(text_bias, ((0, 0), (0, TXT_ROWS - n * TXT_PAD)), constant_values=MASK_FILL).astype(jnp.float32)
        key_bias = jnp.broadcast_to(text_bias.reshape(-1, 1), (TXT_ROWS, LANES))

        bias_all = b_qkv.astype(jnp.float32).reshape(blocks, 2, 3, n, width // n)
        bias_all = lax.dynamic_index_in_dim(bias_all, member, 3, keepdims=False).reshape(blocks, 2, -1)
        gain_all = jnp.stack([q_gain, k_gain], axis=2).astype(jnp.float32).reshape(blocks, 2, 2, n, width // n)
        gain_all = lax.dynamic_index_in_dim(gain_all, member, 3, keepdims=False).reshape(blocks, 2, -1)

        sides = [img, txt]
        for block in range(blocks):
            normed = [modulated_norm(sides[s], mod_all[block, s, 0], mod_all[block, s, 1]) for s in range(2)]
            attended = joint(mesh, normed[0], normed[1], w_qkv, bias_all[block], gain_all[block], key_bias, block, head_dim, 2 + block)
            sides = [modality_out(sides[s], attended[s], mod_all[block, s], w_proj[block, s], b_proj[block, s], w_up[block, s], b_up[block, s], w_down[block, s], b_down[block, s]) for s in range(2)]
        img = sides[0].reshape(slots, run, width)
        txt = sides[1][: slots * txt_run].reshape(slots, txt_run, width)
        return unscatter(mesh, img, txt)

    return jax.shard_map(local_blocks, mesh=mesh, in_specs=(seq_spec, seq_spec, row_spec, row_spec) + (P(),) * 12, out_specs=(seq_spec, seq_spec), check_vma=False)
```

time: 462 us -> 356 us (0.77)
  Pallas kernels: 314 us -> 207 us
    pallas_call x6 -> x2, Pallas kernels: 268 us -> 160 us  [joint(): pl.pallas_call(functools.partial(joint_kernel, n, head_dim, block), out_s...]
where the time goes in v2:
time: 356 us; the launch traced here: 353 us
  Pallas kernels  207 us (58%)
  matrix products  115 us (32%)
  other arithmetic  15.5 us (4%)
  local copies, waits for them, and re-layouts  14.5 us (4%)
    pallas_call x2, Pallas kernels, joint(): pl.pallas_call(functools.partial(joint_kernel, n, head_dim, block), out_s...  160 us
    dot_general x10, matrix products, linear(): jnp.dot(rows, weight, preferred_element_type=jnp.float32)  112 us
    pallas_call x1, Pallas kernels, scatter(): pl.pallas_call(functools.partial(scatter_kernel, n), out_shape=[jax.Shape...  25.9 us
    pallas_call x1, Pallas kernels, unscatter(): pl.pallas_call(functools.partial(unscatter_kernel, n), out_shape=[jax.Sha...  20.9 us

profile of v2, /device:TPU:97, one launch (start us, length us, event | category | flops | bytes accessed | tf_op | source)
XLA Modules:
  0.0 352.9 jit_solution(3031841639353573594)
XLA Ops:
  0.6 1.5 convert_reduce_fusion.6
  2.1 1.4 convert_reduce_fusion.5
  3.5 1.6 copy.23.txt
  5.1 0.8 convert_reduce_fusion.13
  5.9 2.6 fusion.244
  8.5 0.7 copy.24.mod
  9.2 25.9 %scatter.1 = (bf16[8,64,1536]{2,1,0:T(8,128)(2,1)}, bf16[8,5,1536]{2,1,0:T(8,128)(2,1)}, f32[32,9,128]{2,1,0:T(8,128)}) custom-call(bf16[8,64,1536]{2,1,0:T(8,128)(2,1)} %img.1, bf16[8,5,1536]{2,1,0:T(8,128)(2,1)} %copy.23.txt, f32[8,9,128]{2,1,0:T(8,128)} %copy.24.mod), custom_call_target="tpu_custom_call" | custom-call | tf_op jit(solution)/shard_map/scatter/pallas_call | solution.py:89
  35.1 1.1 reshape.384
  36.3 1.7 convert_reduce_fusion.3
  38.1 0.5 multiply_reduce_fusion
  38.8 1.8 fusion.138.img
  40.7 0.1 convert_reduce_fusion.4
  40.8 0.2 fusion.263
  41.0 0.8 fusion.266.txt
  41.9 0.6 copy.33
  42.8 0.6 copy.34
  43.4 0.6 broadcast.450
  44.0 1.4 fusion.320
  45.5 0.1 reshape_squeeze.3
  45.8 0.8 broadcast_in_dim.15.key_bias
  46.5 80.0 %joint.2 = (bf16[512,1536]{1,0:T(8,128)(2,1)}, bf16[48,1536]{1,0:T(8,128)(2,1)}) custom-call(bf16[512,1536]{1,0:T(8,128)(2,1)} %fusion.138.img, bf16[48,1536]{1,0:T(8,128)(2,1)} %fusion.266.txt, bf16[2,2,1536,4608]{3,2,1,0:T(8,128)(2,1)} %w_qkv.3, f32[2,1152]{1,0:T(2,128)} %bitcast.219, f32[2,768]{1,0:T(2,128)} %bitcast.221, ...), custom_call_target="tpu_custom_call" | custom-call | flops 40000000000 | bytes 10000000 | tf_op jit(solution)/shard_map/joint/pallas_call | solution.py:357
  126.6 5.6 %convert_reduce_fusion.2 = (f32[512]{0:T(512)S(1)}, bf16[512,1536]{1,0:T(8,128)(2,1)S(1)}) fusion(f32[1536]{0:T(1024)S(1)} %get-tuple-element.52, bf16[512,1536]{1,0:T(8,128)(2,1)} %get-tuple-element.12, bf16[2,2,1536,1536]{3,2,1,0:T(8,128)(2,1)} %param.26, f32[1536]{0:T(1024)S(1)} %get-tuple-element.39, bf16[512,1536]{1,0:T(8,128)(2,1)S(1)} %bitcast.210), kind=kOutput, calls=%fused_computation.62 | convolution fusion | flops 2421423616 | bytes 9451520 | tf_op jit(solution)/shard_map/dot_general | solution.py:386
  132.2 0.9 slice_reduce_fusion.1
  133.1 0.7 slice_convert_fusion
  133.8 0.5 fusion.128
  134.3 16.9 %fusion.31.clone.7.clone.5 = bf16[512,6144]{1,0:T(8,128)(2,1)S(1)} fusion(bf16[2,2,1536,6144]{3,2,1,0:T(8,128)(2,1)} %param.28, f32[6144]{0:T(1024)S(1)} %bitcast.218, bf16[512,1536]{1,0:T(8,128)(2,1)S(1)} %get-tuple-element.63, f32[1536]{0:T(1024)S(1)} %get-tuple-element.36, ...), kind=kOutput, calls=%fused_computation.33.clone.clone.clone.clone.clone.clone.clone.clone.clone.clone... | convolution fusion | flops 9699852288 | bytes 26779648 | tf_op jit(solution)/shard_map/dot_general | solution.py:386
  151.2 14.3 %convert_reduce_fusion.1 = (f32[512]{0:T(512)S(1)}, bf16[512,1536]{1,0:T(8,128)(2,1)S(1)}) fusion(f32[1536]{0:T(1024)S(1)} %get-tuple-element.48, bf16[2,2,6144,1536]{3,2,1,0:T(8,128)(2,1)} %param.30, bf16[512,1536]{1,0:T(8,128)(2,1)S(1)} %get-tuple-element.63, f32[1536]{0:T(1024)S(1)} %get-tuple-element.38, bf16[512,6144]{1,0:T(8,128)(2,1)S(1)} %fusion.31.clone.7.clone.5), kind=kOutput, calls=%fused_computation.59 | convolution fusion | flops 9669181440 | bytes 28325888 | tf_op jit(solution)/shard_map/dot_general | solution.py:386
  165.6 0.5 fusion.124
  166.1 1.8 fusion.127.img
  167.9 3.4 fusion.325
  171.3 0.2 multiply_reduce_fusion.3
  171.5 15.5 %fusion.326 = (f32[48]{0:T(128)S(1)}, f32[48,1536]{1,0:T(8,128)S(1)}) fusion(f32[48,1536]{1,0:T(8,128)S(1)} %get-tuple-element.67, f32[1536]{0:T(1024)S(1)} %get-tuple-element.47, bf16[2,2,6144,1536]{3,2,1,0:T(8,128)(2,1)} %param.30, bf16[2,2,1536,6144]{3,2,1,0:T(8,128)(2,1)} %param.28, f32[6144]{0:T(1024)S(1)} %bitcast.217, ...), kind=kOutput, calls=%fused_computation.294 | convolution fusion | flops 1815699456 | bytes 38692032 | tf_op jit(solution)/shard_map/dot_general | solution.py:386
  187.0 0.2 multiply_reduce_fusion.2
  187.2 0.8 add_convert_fusion.1.txt
  188.0 0.6 copy.35
  188.6 0.6 copy.36
  189.2 80.0 %joint.3 = (bf16[512,1536]{1,0:T(8,128)(2,1)}, bf16[48,1536]{1,0:T(8,128)(2,1)}) custom-call(bf16[512,1536]{1,0:T(8,128)(2,1)} %fusion.127.img, bf16[48,1536]{1,0:T(8,128)(2,1)} %add_convert_fusion.1.txt, bf16[2,2,1536,4608]{3,2,1,0:T(8,128)(2,1)} %w_qkv.3, f32[2,1152]{1,0:T(2,128)} %bitcast.220, f32[2,768]{1,0:T(2,128)} %bitcast.222, ...), custom_call_target="tpu_custom_call" | custom-call | flops 40000000000 | bytes 10000000 | tf_op jit(solution)/shard_map/joint/pallas_call | solution.py:357
  269.2 5.6 %convert_reduce_fusion = (f32[512]{0:T(512)S(1)}, bf16[512,1536]{1,0:T(8,128)(2,1)S(1)}) fusion(f32[1536]{0:T(1024)S(1)} %copy-done.11, bf16[512,1536]{1,0:T(8,128)(2,1)} %get-tuple-element.14, bf16[2,2,1536,1536]{3,2,1,0:T(8,128)(2,1)} %param.26, f32[1536]{0:T(1024)S(1)} %get-tuple-element.35, bf16[512,1536]{1,0:T(8,128)(2,1)S(1)} %get-tuple-element.65), kind=kOutput, calls=%fused_computation.56 | convolution fusion | flops 2421423616 | bytes 9451520 | tf_op jit(solution)/shard_map/dot_general | solution.py:386
  274.8 0.6 fusion.120
  275.4 16.9 %fusion.39.clone.11 = bf16[512,6144]{1,0:T(8,128)(2,1)S(1)} fusion(bf16[2,2,1536,6144]{3,2,1,0:T(8,128)(2,1)} %param.28, f32[6144]{0:T(1024)S(1)} %bitcast.216, bf16[512,1536]{1,0:T(8,128)(2,1)S(1)} %get-tuple-element.71, f32[1536]{0:T(1024)S(1)} %get-tuple-element.24, f32[512]{0:T(512)S(1)} %add_rsqrt_fusion.1, ...), kind=kOutput, calls=%fused_computation.41.clone.clone.clone.clone.clone.clone.clone.clone.clone.2 | convolution fusion | flops 9699852288 | bytes 26779648 | tf_op jit(solution)/shard_map/dot_general | solution.py:386
  292.4 15.0 %fusion.134 = bf16[512,1536]{1,0:T(8,128)(2,1)} fusion(bf16[512,1536]{1,0:T(8,128)(2,1)S(1)} %get-tuple-element.71, bf16[2,2,6144,1536]{3,2,1,0:T(8,128)(2,1)} %param.30, f32[1536]{0:T(1024)S(1)} %copy-done.10, f32[1536]{0:T(1024)S(1)} %get-tuple-element.26, bf16[512,6144]{1,0:T(8,128)(2,1)S(1)} %fusion.39.clone.11), kind=kOutput, calls=%fused_computation.107 | convolution fusion | flops 9667608576 | bytes 28323840 | tf_op jit(solution)/shard_map/dot_general | solution.py:386
  307.4 3.4 fusion.329
  310.9 0.2 multiply_reduce_fusion.1
  311.1 15.5 %fusion = f32[48,1536]{1,0:T(8,128)S(1)} fusion(bf16[2,2,6144,1536]{3,2,1,0:T(8,128)(2,1)} %param.30, bf16[2,2,1536,6144]{3,2,1,0:T(8,128)(2,1)} %param.28, f32[6144]{0:T(1024)S(1)} %bitcast.215, f32[48,1536]{1,0:T(8,128)S(1)} %get-tuple-element.73, f32[1536]{0:T(1024)S(1)} %copy-done.12, f32[48]{0:T(128)S(1)} %add_rsqrt_fusion.4, ...), kind=kOutput, calls=%fused_computation.2 | convolution fusion | flops 1815257088 | bytes 38375808 | tf_op jit(solution)/shard_map/dot_general | solution.py:386
  326.7 0.7 reshape.391.txt
  327.4 20.9 %unscatter.1 = (bf16[8,64,1536]{2,1,0:T(8,128)(2,1)}, bf16[8,5,1536]{2,1,0:T(8,128)(2,1)}) custom-call(bf16[8,64,1536]{2,1,0:T(8,128)(2,1)} %bitcast.211, bf16[8,5,1536]{2,1,0:T(8,128)(2,1)} %reshape.391.txt), custom_call_target="tpu_custom_call" | custom-call | tf_op jit(solution)/shard_map/unscatter/pallas_call | solution.py:132
  348.3 1.6 copy.29
  350.0 2.7 copy.38
  (70 shorter events, 1.2 us)
Async XLA Ops:
  35.1 3.0 copy-start
  36.3 4.3 %copy-start.1 = (bf16[8,5,1536]{2,1,0:T(8,128)(2,1)S(1)}, bf16[8,5,1536]{2,1,0:T(8,128)(2,1)}, u32[]{:S(2)}) copy-start(bf16[8,5,1536]{2,1,0:T(8,128)(2,1)} %get-tuple-element.11) | copy-start | bytes 368644
  38.0 3.8 %copy-start.3 = (bf16[2,2,4608]{2,1,0:T(2,128)(2,1)S(1)}, bf16[2,2,4608]{2,1,0:T(2,128)(2,1)}, u32[]{:S(2)}) copy-start(bf16[2,2,4608]{2,1,0:T(2,128)(2,1)} %param.23) | copy-start | bytes 110596
  38.0 4.5 %copy-start.7 = (bf16[2,2,24,64]{3,2,1,0:T(8,128)(2,1)S(1)}, bf16[2,2,24,64]{3,2,1,0:T(8,128)(2,1)}, u32[]{:S(2)}) copy-start(bf16[2,2,24,64]{3,2,1,0:T(8,128)(2,1)} %param.25) | copy-start | bytes 36868
  38.1 4.6 %copy-start.8 = (bf16[2,2,24,64]{3,2,1,0:T(8,128)(2,1)S(1)}, bf16[2,2,24,64]{3,2,1,0:T(8,128)(2,1)}, u32[]{:S(2)}) copy-start(bf16[2,2,24,64]{3,2,1,0:T(8,128)(2,1)} %param.24) | copy-start | bytes 36868
  126.6 6.5 %copy-start.2 = (bf16[2,2,6144]{2,1,0:T(2,128)(2,1)S(1)}, bf16[2,2,6144]{2,1,0:T(2,128)(2,1)}, u32[]{:S(2)}) copy-start(bf16[2,2,6144]{2,1,0:T(2,128)(2,1)} %param.29) | copy-start | bytes 147460
  165.6 2.4 copy-start.16
  189.2 80.0 %copy-start.11 = (f32[1536]{0:T(1024)S(1)}, f32[1536]{0:T(1024)}, u32[]{:S(2)}) copy-start(f32[1536]{0:T(1024)} %get-tuple-element.53) | copy-start | bytes 18436
  275.4 16.9 %copy-start.10 = (f32[1536]{0:T(1024)S(1)}, f32[1536]{0:T(1024)}, u32[]{:S(2)}) copy-start(f32[1536]{0:T(1024)} %get-tuple-element.49) | copy-start | bytes 18436
  292.3 15.1 %copy-start.9 = (f32[1536]{0:T(1024)S(1)}, f32[1536]{0:T(1024)}, u32[]{:S(2)}) copy-start(f32[1536]{0:T(1024)} %get-tuple-element.50) | copy-start | bytes 18436
  292.4 15.1 %copy-start.14 = (f32[1536]{0:T(1024)S(1)}, f32[1536]{0:T(1024)}, u32[]{:S(2)}) copy-start(f32[1536]{0:T(1024)} %get-tuple-element.23) | copy-start | bytes 18436
  292.4 15.1 %copy-start.15 = (bf16[48,1536]{1,0:T(8,128)(2,1)S(1)}, bf16[48,1536]{1,0:T(8,128)(2,1)}, u32[]{:S(2)}) copy-start(bf16[48,1536]{1,0:T(8,128)(2,1)} %get-tuple-element.15) | copy-start | bytes 442372
  307.4 3.7 %copy-start.6 = (f32[1,1,6144]{2,1,0:T(1,128)S(1)}, f32[1,1,6144]{2,1,0:T(1,128)}, u32[]{:S(2)}) copy-start(f32[1,1,6144]{2,1,0:T(1,128)} %get-tuple-element.56) | copy-start | bytes 73732
  307.4 3.7 %copy-start.12 = (f32[1536]{0:T(1024)S(1)}, f32[1536]{0:T(1024)}, u32[]{:S(2)}) copy-start(f32[1536]{0:T(1024)} %get-tuple-element.21) | copy-start | bytes 18436
  307.4 3.7 %copy-start.13 = (f32[1536]{0:T(1024)S(1)}, f32[1536]{0:T(1024)}, u32[]{:S(2)}) copy-start(f32[1536]{0:T(1024)} %get-tuple-element.22) | copy-start | bytes 18436
  311.1 15.5 %copy-start.4 = (f32[1536]{0:T(1024)S(1)}, f32[1536]{0:T(1024)}, u32[]{:S(2)}) copy-start(f32[1536]{0:T(1024)} %get-tuple-element.46) | copy-start | bytes 18436
  311.1 15.5 %copy-start.5 = (f32[1536]{0:T(1024)S(1)}, f32[1536]{0:T(1024)}, u32[]{:S(2)}) copy-start(f32[1536]{0:T(1024)} %get-tuple-element.20) | copy-start | bytes 18436

commit v3 on v2

--- a/solution.py
+++ b/solution.py
@@ -17,6 +17,9 @@
 TXT_ROWS = 256
 Q_BLOCK = 768
 K_BLOCK = 256
+MLP_TILE = 1024
+ROW_BLOCK = 512
+NORM_ROWS = 128
 
 
 def place():
@@ -32,11 +35,21 @@
     return pltpu.make_async_remote_copy(src_ref=src, dst_ref=dst, send_sem=send, recv_sem=recv, device_id={'r': r, 'u': u}, device_id_type=MESH)
 
 
+def hello(peers):
+    for r, u in peers:
+        pl.semaphore_signal(pltpu.get_barrier_semaphore(), inc=1, device_id={'r': r, 'u': u}, device_id_type=MESH)
+
+
 def greet(peers, count):
-    barrier = pltpu.get_barrier_semaphore()
-    for r, u in peers:
-        pl.semaphore_signal(barrier, inc=1, device_id={'r': r, 'u': u}, device_id_type=MESH)
-    pl.semaphore_wait(barrier, count)
+    hello(peers)
+    pl.semaphore_wait(pltpu.get_barrier_semaphore(), count)
+
+
+def modulated_norm(hidden, shift, scale):
+    wide = hidden.astype(jnp.float32)
+    centered = wide - jnp.mean(wide, axis=-1, keepdims=True)
+    variance = jnp.mean(centered * centered, axis=-1, keepdims=True)
+    return ((1.0 + scale) * (centered * lax.rsqrt(variance + EPSILON)) + shift).astype(jnp.bfloat16)
 
 
 def scatter_kernel(n, img, txt, mod, img_o, txt_o, mod_o, send, recv, mod_send, mod_recv, local):
@@ -151,12 +164,13 @@
     return me, peer
 
 
-def joint_kernel(n, head_dim, block, img, txt, w_qkv, bias, gain, key_bias, img_o, txt_o, a_img, a_txt, w_i, w_t, q_s, k_s, v_s, s_a, s_b, o_s, send, recv, o_send, o_recv, local):
+def joint_kernel(n, head_dim, block, x_img, x_txt, mod, w_qkv, bias, gain, key_bias, img_o, txt_o, a_img, a_txt, w_i, w_t, q_s, k_s, v_s, s_a, s_b, o_s, send, recv, o_send, o_recv, local):
     me, peer = ring_place(n)
     right, left = peer(1), peer(-1)
-    rows, width = img.shape
-    txt_rows = txt.shape[0]
+    rows, width = x_img.shape
+    txt_rows = x_txt.shape[0]
     img_rows = n * rows
+    img, txt = a_img.at[me], a_txt.at[me]
     pairs, all_rows = q_s.shape[:2]
     cols = pairs * LANES
     weights = []
@@ -166,10 +180,17 @@
             weights.append(pltpu.make_async_copy(w_qkv.at[block, side, :, pl.ds(start, cols)], ref.at[:, pl.ds(t * cols, cols)], local.at[2 + 3 * side + t]))
     for copy in weights:
         copy.start()
-    mine = [pltpu.make_async_copy(img, a_img.at[me], local.at[0]), pltpu.make_async_copy(txt, a_txt.at[me], local.at[1])]
-    for copy in mine:
-        copy.start()
-    greet([peer(d) for d in range(1, n)], n - 1)
+    hello([peer(d) for d in range(1, n)])
+    for side, (source, target) in enumerate(((x_txt, a_txt), (x_img, a_img))):
+        side = 1 - side
+        size = min(source.shape[0], NORM_ROWS)
+
+        @pl.loop(0, source.shape[0] // size)
+        def _(step):
+            span = pl.ds(pl.multiple_of(step * size, size), size)
+            target[me, span, :] = modulated_norm(source[span, :], mod[side, 0:1, :], mod[side, 1:2, :])
+
+    pl.semaphore_wait(pltpu.get_barrier_semaphore(), n - 1)
     piece = rows // 4
     lside, rside, far = (me + n - 1) % n, (me + 1) % n, (me + 2) % n
 
@@ -226,7 +247,7 @@
                         v_s[p, :, pl.ds(start, size)] = value[:, offset:offset + size]
                     offset += size
 
-    for copy in weights + mine:
+    for copy in weights:
         copy.wait()
     half_rows = rows // 2
 
@@ -346,7 +367,7 @@
                 copy.wait_recv()
 
 
-def joint(mesh, img, txt, w_qkv, bias, gain, key_bias, block, head_dim, collective_id):
+def joint(mesh, img, txt, mod, w_qkv, bias, gain, key_bias, block, head_dim, collective_id):
     n = mesh.shape['u']
     width = img.shape[1]
     all_rows = n * img.shape[0] + TXT_ROWS
@@ -357,7 +378,7 @@
     return pl.pallas_call(
         functools.partial(joint_kernel, n, head_dim, block),
         out_shape=[jax.ShapeDtypeStruct(img.shape, bf16), jax.ShapeDtypeStruct(txt.shape, bf16)],
-        in_specs=[vmem, vmem, pl.BlockSpec(memory_space=pl.ANY), vmem, vmem, vmem],
+        in_specs=[vmem, vmem, vmem, pl.BlockSpec(memory_space=pl.ANY), vmem, vmem, vmem],
         out_specs=[vmem, vmem],
         scratch_shapes=[
             pltpu.VMEM((n,) + img.shape, bf16), pltpu.VMEM((n,) + txt.shape, bf16),
@@ -372,26 +393,71 @@
         compiler_params=pltpu.CompilerParams(collective_id=collective_id, has_side_effects=True, vmem_limit_bytes=60 * 2**20),
         cost_estimate=pl.CostEstimate(flops=4 * 10**10, bytes_accessed=10**7, transcendentals=0),
         name='joint',
-    )(img, txt, w_qkv, bias, gain, key_bias)
-
-
-def modulated_norm(hidden, shift, scale):
-    wide = hidden.astype(jnp.float32)
-    centered = wide - jnp.mean(wide, axis=-1, keepdims=True)
-    variance = jnp.mean(centered * centered, axis=-1, keepdims=True)
-    return ((1.0 + scale) * (centered * lax.rsqrt(variance + EPSILON)) + shift).astype(jnp.bfloat16)
-
-
-def linear(rows, weight, bias):
-    return jnp.dot(rows, weight, preferred_element_type=jnp.float32) + bias.astype(jnp.float32)
-
-
-def modality_out(hidden, attended, mod, w_proj, b_proj, w_up, b_up, w_down, b_down):
-    residual = hidden.astype(jnp.float32) + mod[2] * linear(attended, w_proj, b_proj)
-    hidden = residual.astype(jnp.bfloat16)
-    normed = modulated_norm(hidden, mod[3], mod[4])
-    inner = jax.nn.gelu(linear(normed, w_up, b_up), approximate=True).astype(jnp.bfloat16)
-    return (hidden.astype(jnp.float32) + mod[5] * linear(inner, w_down, b_down)).astype(jnp.bfloat16)
+    )(img, txt, mod, w_qkv, bias, gain, key_bias)
+
+
+def mlp_kernel(x_i, x_t, o_i, o_t, mod, wp_i, wp_t, wu_i, wu_t, wd_i, wd_t, bias, bias_up_i, bias_up_t, y_i, y_t, r_i, r_t, a_i, a_t, acc_i, acc_t):
+    outs = (y_i, y_t)
+    step = pl.program_id(0)
+    tiles = pl.num_programs(0)
+    sides = ((x_i, o_i, wp_i, wu_i, wd_i, bias_up_i, r_i, a_i, acc_i), (x_t, o_t, wp_t, wu_t, wd_t, bias_up_t, r_t, a_t, acc_t))
+
+    def row(ref, side, k):
+        return ref[side, k:k + 1, :]
+
+    def row_blocks(ref):
+        size = min(ref.shape[0], ROW_BLOCK)
+        return [pl.ds(start, size) for start in range(0, ref.shape[0], size)]
+
+    @pl.when(step == 0)
+    def _():
+        for side, (x, o, wp, wu, wd, bu, r, a, acc) in enumerate(sides):
+            for span in row_blocks(x):
+                lin = jnp.dot(o[span, :], wp[0, 0], preferred_element_type=jnp.float32) + bias[side, 0:1, :]
+                hidden = (x[span, :].astype(jnp.float32) + row(mod, side, 2) * lin).astype(jnp.bfloat16)
+                r[span, :] = hidden
+                a[span, :] = modulated_norm(hidden, row(mod, side, 3), row(mod, side, 4))
+                acc[span, :] = jnp.zeros_like(acc[span, :])
+
+    for side, (x, o, wp, wu, wd, bu, r, a, acc) in enumerate(sides):
+        for span in row_blocks(x):
+            inner = jnp.dot(a[span, :], wu[0, 0], preferred_element_type=jnp.float32) + bu[0]
+            inner = jax.nn.gelu(inner, approximate=True).astype(jnp.bfloat16)
+            acc[span, :] += jnp.dot(inner, wd[0, 0], preferred_element_type=jnp.float32)
+
+    @pl.when(step == tiles - 1)
+    def _():
+        for side, (x, o, wp, wu, wd, bu, r, a, acc) in enumerate(sides):
+            for span in row_blocks(x):
+                lin = acc[span, :] + bias[side, 1:2, :]
+                hidden = (r[span, :].astype(jnp.float32) + row(mod, side, 5) * lin).astype(jnp.bfloat16)
+                outs[side][span, :] = hidden
+
+
+def mlp(sides, attended, mod, w_proj, b_proj, w_up, b_up, w_down, b_down, block):
+    width, inner = w_up.shape[2:]
+    tiles = inner // MLP_TILE
+    bias = jnp.stack([b_proj[block], b_down[block]], axis=1).astype(jnp.float32)
+    bias_up = b_up.astype(jnp.float32).reshape(-1, 1, inner)
+    whole = lambda shape: pl.BlockSpec(shape, lambda t: (0,) * len(shape))
+    sizes = [sides[0].shape, sides[1].shape]
+    wp = [pl.BlockSpec((1, 1, width, width), lambda t, s=s: (block, s, 0, 0)) for s in range(2)]
+    wu = [pl.BlockSpec((1, 1, width, MLP_TILE), lambda t, s=s: (block, s, 0, t)) for s in range(2)]
+    wd = [pl.BlockSpec((1, 1, MLP_TILE, width), lambda t, s=s: (block, s, t, 0)) for s in range(2)]
+    bu = [pl.BlockSpec((1, 1, MLP_TILE), lambda t, s=s: (block * 2 + s, 0, t)) for s in range(2)]
+    shapes = [jax.ShapeDtypeStruct(size, jnp.bfloat16) for size in sizes]
+    scratch = [pltpu.VMEM(size, dtype) for dtype in (jnp.bfloat16, jnp.bfloat16, jnp.float32) for size in sizes]
+    return pl.pallas_call(
+        mlp_kernel,
+        out_shape=shapes,
+        grid=(tiles,),
+        in_specs=[whole(s) for s in sizes] * 2 + [whole(mod.shape)] + wp + wu + wd + [whole(bias.shape)] + bu,
+        out_specs=[whole(s.shape) for s in shapes],
+        scratch_shapes=scratch,
+        compiler_params=pltpu.CompilerParams(vmem_limit_bytes=60 * 2**20, dimension_semantics=('arbitrary',)),
+        cost_estimate=pl.CostEstimate(flops=25 * 10**9, bytes_accessed=86 * 10**6, transcendentals=0),
+        name='mlp',
+    )(sides[0], sides[1], attended[0], attended[1], mod, w_proj, w_proj, w_up, w_up, w_down, w_down, bias, bias_up, bias_up)
 
 
 def solution(mesh):
@@ -416,7 +482,7 @@
         b_mine = lax.dynamic_slice(b_mod, (which // 2, which % 2, col), (1, 1, per))[0, 0]
         mod_mine = jnp.dot(silu_vec, w_mine, preferred_element_type=jnp.float32) + b_mine.astype(jnp.float32)
         img, txt, mod_all = scatter(mesh, image, text, mod_mine.reshape(-1, per // LANES, LANES))
-        mod_all = mod_all.reshape(blocks, 2, 6, 1, width)
+        mod_all = mod_all.reshape(blocks, 2, 6, width)
         slots, run, _ = img.shape
         txt_run = txt.shape[1]
         img = img.reshape(slots * run, width)
@@ -436,9 +502,8 @@
 
         sides = [img, txt]
         for block in range(blocks):
-            normed = [modulated_norm(sides[s], mod_all[block, s, 0], mod_all[block, s, 1]) for s in range(2)]
-            attended = joint(mesh, normed[0], normed[1], w_qkv, bias_all[block], gain_all[block], key_bias, block, head_dim, 2 + block)
-            sides = [modality_out(sides[s], attended[s], mod_all[block, s], w_proj[block, s], b_proj[block, s], w_up[block, s], b_up[block, s], w_down[block, s], b_down[block, s]) for s in range(2)]
+            attended = joint(mesh, sides[0], sides[1], mod_all[block], w_qkv, bias_all[block], gain_all[block], key_bias, block, head_dim, 2 + block)
+            sides = mlp(sides, attended, mod_all[block], w_proj, b_proj, w_up, b_up, w_down, b_down, block)
         img = sides[0].reshape(slots, run, width)
         txt = sides[1][: slots * txt_run].reshape(slots, txt_run, width)
         return unscatter(mesh, img, txt)

time: 356 us -> 327 us (0.919)
  matrix products: 115 us -> 2.59 us
  Pallas kernels: 207 us -> 297 us
  other arithmetic: 15.5 us -> 2.08 us
  local copies, waits for them, and re-layouts: 14.5 us -> 20.7 us
    dot_general x10 -> x0, matrix products: 112 us -> none  [linear(): jnp.dot(rows, weight, preferred_element_type=jnp.float32)]
    pallas_call x0 -> x2, Pallas kernels: none -> 90.3 us  [mlp(): pl.pallas_call(mlp_kernel, out_shape=shapes, grid=(tiles,), in_specs=[who...]
    convert_element_type x8 -> x2, other arithmetic: 8.79 us -> 1.27 us  [mlp(): bias = jnp.stack([b_proj[block], b_down[block]], axis=1).astype(jnp.float32)]
    reduce_sum x10 -> x0, other arithmetic: 4.86 us -> none  [the longest x8 3.01 us: modulated_norm(): variance = jnp.mean(centered * centered, axis=-1, keepdims=True)]
where the time goes in v3:
time: 327 us; the launch traced here: 323 us
  Pallas kernels  297 us (91%)
  local copies, waits for them, and re-layouts  20.7 us (6%)
    pallas_call x2, Pallas kernels, joint(): pl.pallas_call(functools.partial(joint_kernel, n, head_dim, block), out_s...  160 us
    pallas_call x2, Pallas kernels, mlp(): pl.pallas_call(mlp_kernel, out_shape=shapes, grid=(tiles,), in_specs=[who...  90.3 us
    pallas_call x1, Pallas kernels, scatter(): pl.pallas_call(functools.partial(scatter_kernel, n), out_shape=[jax.Shape...  25.9 us
    pallas_call x1, Pallas kernels, unscatter(): pl.pallas_call(functools.partial(unscatter_kernel, n), out_shape=[jax.Sha...  20.3 us

profile of v3, /device:TPU:97, one launch (start us, length us, event | category | flops | bytes accessed | tf_op | source)
XLA Modules:
  0.0 323.3 jit_solution(3663386691690253421)
XLA Ops:
  0.6 0.0 copy-start.1
  0.6 0.0 copy-start.2
  0.7 0.0 copy-start
  0.8 0.5 broadcast.23
  1.3 1.4 fusion.20
  2.6 0.1 squeeze.35
  2.7 0.8 convert_reduce_fusion
  3.5 0.8 stack.15
  4.4 0.8 stack.16
  5.3 0.6 copy.40
  5.9 0.6 copy.38
  6.4 0.7 slice_bitcast_fusion.3
  7.2 0.7 slice_bitcast_fusion.2
  7.9 0.6 maximum_convert_fusion.1.bias
  8.6 0.6 maximum_convert_fusion.bias
  9.2 0.1 reshape_squeeze.3
  9.4 0.1 reshape.76
  9.5 0.1 reshape.77
  9.6 2.6 fusion.6
  12.1 0.7 copy.24.mod
  12.8 0.0 copy-done.2
  12.8 0.1 dynamic-slice_reduce_fusion
  12.9 0.6 copy.39
  13.5 0.6 copy.37
  14.1 0.0 copy-done.1
  14.1 0.7 reshape.86.bias_up_i.bias_up_t
  14.9 0.7 broadcast_in_dim.19.key_bias
  15.6 0.0 copy-done
  15.6 0.7 copy.23.txt
  16.3 25.9 %scatter.1 = (bf16[8,64,1536]{2,1,0:T(8,128)(2,1)}, bf16[8,5,1536]{2,1,0:T(8,128)(2,1)}, f32[32,9,128]{2,1,0:T(8,128)}) custom-call(bf16[8,64,1536]{2,1,0:T(8,128)(2,1)} %img.1, bf16[8,5,1536]{2,1,0:T(8,128)(2,1)} %copy.23.txt, f32[8,9,128]{2,1,0:T(8,128)} %copy.24.mod), custom_call_target="tpu_custom_call" | custom-call | tf_op jit(solution)/shard_map/scatter/pallas_call | solution.py:102
  42.3 1.0 reshape.73
  43.3 0.7 pad.12.x_txt.x_t
  43.9 1.0 fusion.21
  44.9 0.7 squeeze.36.mod
  45.6 0.7 squeeze.32.mod
  46.2 79.7 %joint.2 = (bf16[512,1536]{1,0:T(8,128)(2,1)}, bf16[48,1536]{1,0:T(8,128)(2,1)}) custom-call(bf16[512,1536]{1,0:T(8,128)(2,1)} %bitcast.40, bf16[48,1536]{1,0:T(8,128)(2,1)} %pad.12.x_txt.x_t, f32[2,6,1536]{2,1,0:T(8,128)} %squeeze.32.mod, bf16[2,2,1536,4608]{3,2,1,0:T(8,128)(2,1)} %w_qkv.3, f32[2,1152]{1,0:T(2,128)} %bitcast.47, f32[2,768]{1,0:T(2,128)} %bitcast.49, ...), custom_call_target="tpu_custom_call" | custom-call | flops 40000000000 | bytes 10000000 | tf_op jit(solution)/shard_map/joint/pallas_call | solution.py:378
  125.9 45.2 %mlp.2 = (bf16[512,1536]{1,0:T(8,128)(2,1)}, bf16[48,1536]{1,0:T(8,128)(2,1)}) custom-call(bf16[512,1536]{1,0:T(8,128)(2,1)} %bitcast.41, bf16[48,1536]{1,0:T(8,128)(2,1)} %pad.12.x_txt.x_t, bf16[512,1536]{1,0:T(8,128)(2,1)} %get-tuple-element.16.o_i, bf16[48,1536]{1,0:T(8,128)(2,1)} %get-tuple-element.17.o_t, f32[2,6,1536]{2,1,0:T(8,128)} %squeeze.32.mod, ...), custom_call_target="tpu_custom_call" | custom-call | flops 24999999488 | bytes 86000000 | tf_op jit(solution)/shard_map/mlp/pallas_call | solution.py:450
  171.1 80.3 %joint.3 = (bf16[512,1536]{1,0:T(8,128)(2,1)}, bf16[48,1536]{1,0:T(8,128)(2,1)}) custom-call(bf16[512,1536]{1,0:T(8,128)(2,1)} %get-tuple-element.18.x_img.x_i, bf16[48,1536]{1,0:T(8,128)(2,1)} %get-tuple-element.19.x_txt.x_t, f32[2,6,1536]{2,1,0:T(8,128)} %squeeze.36.mod, bf16[2,2,1536,4608]{3,2,1,0:T(8,128)(2,1)} %w_qkv.3, f32[2,1152]{1,0:T(2,128)} %bitcast.46, ...), custom_call_target="tpu_custom_call" | custom-call | flops 40000000000 | bytes 10000000 | tf_op jit(solution)/shard_map/joint/pallas_call | solution.py:378
  251.5 45.1 %mlp.3 = (bf16[512,1536]{1,0:T(8,128)(2,1)}, bf16[48,1536]{1,0:T(8,128)(2,1)}) custom-call(bf16[512,1536]{1,0:T(8,128)(2,1)} %get-tuple-element.18.x_img.x_i, bf16[48,1536]{1,0:T(8,128)(2,1)} %get-tuple-element.19.x_txt.x_t, bf16[512,1536]{1,0:T(8,128)(2,1)} %get-tuple-element.20.o_i, bf16[48,1536]{1,0:T(8,128)(2,1)} %get-tuple-element.21.o_t, ...), custom_call_target="tpu_custom_call" | custom-call | flops 24999999488 | bytes 86000000 | tf_op jit(solution)/shard_map/mlp/pallas_call | solution.py:450
  296.6 0.9 slice.51
  297.5 0.7 reshape.81.txt
  298.2 20.3 %unscatter.1 = (bf16[8,64,1536]{2,1,0:T(8,128)(2,1)}, bf16[8,5,1536]{2,1,0:T(8,128)(2,1)}) custom-call(bf16[8,64,1536]{2,1,0:T(8,128)(2,1)} %bitcast.42, bf16[8,5,1536]{2,1,0:T(8,128)(2,1)} %reshape.81.txt), custom_call_target="tpu_custom_call" | custom-call | tf_op jit(solution)/shard_map/unscatter/pallas_call | solution.py:145
  318.6 1.6 copy.33
  320.2 2.7 copy.42
  (13 shorter events, 0.2 us)
Async XLA Ops:
  0.6 13.5 %copy-start.1 = (bf16[2,2,6144]{2,1,0:T(2,128)(2,1)S(1)}, bf16[2,2,6144]{2,1,0:T(2,128)(2,1)}, u32[]{:S(2)}) copy-start(bf16[2,2,6144]{2,1,0:T(2,128)(2,1)} %param.29) | copy-start | bytes 147460
  0.6 12.2 %copy-start.2 = (bf16[2,2,4608]{2,1,0:T(2,128)(2,1)S(1)}, bf16[2,2,4608]{2,1,0:T(2,128)(2,1)}, u32[]{:S(2)}) copy-start(bf16[2,2,4608]{2,1,0:T(2,128)(2,1)} %param.23) | copy-start | bytes 110596
  0.7 15.0 %copy-start = (bf16[8,5,1536]{2,0,1:T(8,128)(2,1)S(1)}, bf16[8,5,1536]{2,0,1:T(8,128)(2,1)}, u32[]{:S(2)}) copy-start(bf16[8,5,1536]{2,0,1:T(8,128)(2,1)} %param.17) | copy-start | bytes 368644
